TPU v7x, 512 devices: a whole 4x8x8 slice. The times are simulated.
512 devices in a mesh: blk: 32 (over z, y_lo), head: 16 (over x, y_hi, core).
Axes of the slice: x: 4, y: 8 (y_hi: 2, y_lo: 4; y = y_hi * 4 + y_lo), z: 8, core: 2. Of those that a mesh axis runs over, the one named last changes fastest.
Arguments:
- queries: bfloat16 [16384, 1024], P('blk', 'head'), may hold values from -170 to 170
- key_rows: bfloat16 [16384, 1024], P('blk', 'head'), may hold values from -9 to 9
- values: bfloat16 [16384, 1024], P('blk', 'head'), may hold values from -48 to 48
- text_keys: bfloat16 [1232, 1024], P(None, 'head'), may hold values from -9 to 9
- text_values: bfloat16 [1232, 1024], P(None, 'head'), may hold values from -48 to 48
- block_image: int32 [128], replicated, may hold values from 0 to 7, as said below
- gate_image: float32 [8, 1536], replicated, may hold values from 0.5 to 2
- residual: bfloat16 [16384, 1536], P(('blk', 'head')), may hold values from -6 to 6
- w_out: bfloat16 [1024, 1536], P('head'), may hold values from -0.1875 to 0.1875
Outputs:
- stream_out: bfloat16 [16384, 1536], P(('blk', 'head'))
Inputs may be any that keep to these rules, and one draw needn't show every extreme that they name: `block_image`: each image number 0 to 7 names 8 to 24 of the entries, some image exactly 24 and some exactly 8; the blocks of an image lie anywhere in the array.
All inputs are finite; a program needn't handle non-finite values.
Results may differ from a plain program's by a relative error of at most 0.014.
Values may be sent and summed in bfloat16 or wider, within the bound.
A program may use at most 64 MiB of HBM per device.

v0:
```python
import math

import jax
import jax.numpy as jnp
from jax import lax
from jax.sharding import PartitionSpec as P

HD = 64
TEXT = 154
BS = 128


neg_large = -1e30


def side_by_side(arrays, axis, dim, along):
    widths = [a.shape[along] for a in arrays]
    both = jnp.concatenate(arrays, axis=along)
    result = lax.all_gather(both, axis, axis=dim, tiled=True)
    return tuple(jnp.split(result, [sum(widths[:k]) for k in range(1, len(widths))], axis=along))


def absorb(running, query_three, query_image, key_slab, value_slab, key_image):
    best, total, accum = running
    heads = query_three.shape[1]
    width = query_three.shape[2]
    key_three = key_slab.reshape(key_slab.shape[0], heads, width)
    value_three = value_slab.reshape(value_slab.shape[0], heads, width)
    scores = jnp.einsum("qhd,khd->hqk", query_three, key_three, preferred_element_type=jnp.float32)
    scores = scores * (1.0 / math.sqrt(width))
    allowed = query_image[:, None] == key_image[None, :]
    scores = jnp.where(allowed[None], scores, neg_large)
    newbest = jnp.maximum(best, jnp.max(scores, axis=2))
    weights = jnp.exp(scores - newbest[..., None])
    shrink = jnp.exp(best - newbest)
    total = total * shrink + jnp.sum(weights, axis=2)
    update = jnp.einsum(
        "hqk,khd->hqd",
        weights.astype(jnp.bfloat16),
        value_three,
        preferred_element_type=jnp.float32,
    )
    accum = accum * shrink[..., None] + update
    return (newbest, total, accum)


def on_device(
    queries, key_rows, values, text_keys, text_values, block_image, gate_image, residual, w_out
):
    tok_blk = queries.shape[0]
    ncols = queries.shape[1]
    heads_here = ncols // HD
    blocks_here = tok_blk // BS
    token_image = jnp.repeat(block_image, BS)
    blk_index = lax.axis_index("blk")
    my_blocks = lax.dynamic_slice_in_dim(block_image, blk_index * blocks_here, blocks_here)
    query_image = jnp.repeat(my_blocks, BS)
    text_image = jnp.arange(text_keys.shape[0]) // TEXT
    start_state = (
        jnp.full((heads_here, tok_blk), neg_large, jnp.float32),
        jnp.zeros((heads_here, tok_blk), jnp.float32),
        jnp.zeros((heads_here, tok_blk, HD), jnp.float32),
    )
    query_three = queries.reshape(tok_blk, heads_here, HD)
    running = absorb(start_state, query_three, query_image, text_keys, text_values, text_image)
    fold_running = running
    key_piece, value_piece = side_by_side((key_rows, values), "blk", 0, 1)
    length = key_piece.shape[0]

    def advance(state, position):
        begin = position * tok_blk
        key_slab = lax.dynamic_slice_in_dim(key_piece, begin, tok_blk)
        value_slab = lax.dynamic_slice_in_dim(value_piece, begin, tok_blk)
        slab_image = lax.dynamic_slice_in_dim(token_image, begin, tok_blk)
        return (absorb(state, query_three, query_image, key_slab, value_slab, slab_image), None)

    fold_running, unused = lax.scan(
        advance, fold_running, jnp.arange(length // tok_blk, dtype=jnp.int32)
    )
    best, total, accum = fold_running
    attended = (accum / total[..., None]).astype(jnp.bfloat16)
    attended = attended.transpose(1, 0, 2).reshape(tok_blk, ncols)
    tok_dev = tok_blk // lax.axis_size("head")
    mixed = lax.all_to_all(attended, "head", split_axis=0, concat_axis=1, tiled=True)
    projected = jnp.dot(
        mixed, lax.all_gather(w_out, "head", axis=0, tiled=True), preferred_element_type=jnp.float32
    )
    head_index = lax.axis_index("head")
    row_image = lax.dynamic_slice_in_dim(query_image, head_index * tok_dev, tok_dev)
    onehot = (
        row_image[:, None] == jnp.arange(gate_image.shape[0], dtype=jnp.int32)[None, :]
    ).astype(jnp.float32)
    gating = jnp.dot(onehot, gate_image, precision=lax.Precision.HIGHEST)
    return (residual.astype(jnp.float32) + gating * projected).astype(jnp.bfloat16)


def solution(mesh):
    placed = (
        P("blk", "head"),
        P("blk", "head"),
        P("blk", "head"),
        P(None, "head"),
        P(None, "head"),
        P(),
        P(),
        P(("blk", "head"), None),
        P("head", None),
    )
    return jax.shard_map(
        on_device, mesh=mesh, in_specs=placed, out_specs=P(("blk", "head"), None), check_vma=False
    )
```

profile of v0, /device:TPU:1, one launch (start us, length us, event | category | flops | bytes accessed | tf_op | source)
XLA Modules:
  0.0 353.7 jit_solution(8619565113360705211)
XLA Ops:
  11.6 1.5 fusion.35
  14.2 148.3 %all-gather.3.cloned.1.call-done = bf16[16384,128]{1,0:T(8,128)(2,1)} async-done(((bf16[512,128]{1,0:T(8,128)(2,1)}), bf16[16384,128]{1,0:T(8,128)(2,1)}) %all-gather.3.cloned.1.call-update) | async-done | bytes 4194320 | tf_op jit(solution)/shard_map/all_gather | solution.py:19
  162.5 7.3 %fusion.34 = (bf16[16384,64]{1,0:T(8,128)(2,1)}, bf16[16384,64]{1,0:T(8,128)(2,1)}) fusion(bf16[16384,128]{1,0:T(8,128)(2,1)} %all-gather.3.cloned.1.call-done), kind=kLoop, calls=%fused_computation.48 | loop fusion | bytes 8388608 | tf_op jit(solution)/shard_map/split | solution.py:20
  169.9 133.4 %while.15 = (s32[]{:T(128)}, f32[1,512]{1,0:T(1,128)S(1)}, f32[1,512]{1,0:T(1,128)S(1)}, f32[1,512,64]{1,2,0:T(8,128)S(1)}, s32[32]{0:T(128)S(1)}, /*index=5*/s3...) while((s32[]{:T(128)}, f32[1,512]{1,0:T(1,128)S(1)}, ...), condition=%wide.region_5.6_spmd.clone, body=%wide.region_2.5_spmd.clone.sunk | while | flops 69272576 | bytes 3778779 | solution.py:77
  172.8 1.2 fusion.51
  181.1 1.2 fusion.51
  185.3 1.2 fusion.51
  189.4 1.2 fusion.51
  197.8 1.2 fusion.51
  201.9 1.2 fusion.51
  206.1 1.2 fusion.51
  210.3 1.2 fusion.51
  214.4 1.2 fusion.51
  218.6 1.2 fusion.51
  226.9 1.2 fusion.51
  231.1 1.2 fusion.51
  235.3 1.2 fusion.51
  243.6 1.2 fusion.51
  247.8 1.2 fusion.51
  252.0 1.3 fusion.51
  264.5 1.2 fusion.51
  304.3 29.3 %all-to-all-start = ((bf16[16,2,1024]{2,1,0:T(2,128)(2,1)}), bf16[16,2,1024]{2,1,0:T(2,128)(2,1)S(1)}, u32[]{:S(2)}, u32[]{:S(2)}) async-start(bf16[16,2,1024]{2,1,0:T(2,128)(2,1)} %reshape.134), calls=%async_computation | async-start | bytes 131072 | tf_op jit(solution)/shard_map/all_to_all | solution.py:84
  333.8 9.4 %all-to-all-done = bf16[16,2,1024]{2,1,0:T(2,128)(2,1)S(1)} async-done(((bf16[16,2,1024]{2,1,0:T(2,128)(2,1)}), bf16[16,2,1024]{2,1,0:T(2,128)(2,1)S(1)}, u32[]{:S(2)}, u32[]{:S(2)}) %all-to-all-start) | async-done | bytes 65568 | tf_op jit(solution)/shard_map/all_to_all | solution.py:84
  343.7 3.2 fusion.16
  (306 shorter events, 97.0 us)
Async XLA Ops:
  6.5 5.1 %copy-start = (bf16[1232,64]{0,1:T(8,128)(2,1)S(1)}, bf16[1232,64]{0,1:T(8,128)(2,1)}, u32[]{:S(2)}) copy-start(bf16[1232,64]{0,1:T(8,128)(2,1)} %param.14) | copy-start | bytes 473092
  6.5 155.9 %all-gather.3.cloned.1.call-start = ((), (), s32[]{:S(2)}) async-start(), calls=%async_computation.1 | async-start | bytes 4325376 | tf_op jit(solution)/shard_map/all_gather | solution.py:19
  9.3 334.4 %all-gather.5.cloned.1.call-start = ((), (), s32[]{:S(2)}) async-start(), calls=%async_computation.2 | async-start | bytes 3342336 | tf_op jit(solution)/shard_map/all_gather | solution.py:86
  11.6 2.0 copy-start.1
  14.2 155.6 %copy-start.4 = (bf16[512,64]{0,1:T(8,128)(2,1)S(1)}, bf16[512,64]{0,1:T(8,128)(2,1)}, u32[]{:S(2)}) copy-start(bf16[512,64]{0,1:T(8,128)(2,1)} %param.11) | copy-start | bytes 196612
  169.8 163.7 %copy-start.3 = (f32[8,1536]{1,0:T(8,128)S(1)}, f32[8,1536]{1,0:T(8,128)}, u32[]{:S(2)}) copy-start(f32[8,1536]{1,0:T(8,128)} %param.17) | copy-start | bytes 147460
  169.8 173.8 %copy-start.2 = (bf16[32,1536]{1,0:T(8,128)(2,1)S(1)}, bf16[32,1536]{1,0:T(8,128)(2,1)}, u32[]{:S(2)}) copy-start(bf16[32,1536]{1,0:T(8,128)(2,1)} %param.18) | copy-start | bytes 294916
  304.3 39.0 %all-to-all-start = ((bf16[16,2,1024]{2,1,0:T(2,128)(2,1)}), bf16[16,2,1024]{2,1,0:T(2,128)(2,1)S(1)}, u32[]{:S(2)}, u32[]{:S(2)}) async-start(bf16[16,2,1024]{2,1,0:T(2,128)(2,1)} %reshape.134), calls=%async_computation | async-start | bytes 131072 | tf_op jit(solution)/shard_map/all_to_all | solution.py:84
Sparse Core Ops, SparseCore 0:
  9.4 153.0 all-gather.2
  165.8 94.2 all-gather.4
where the time goes:
time: 355 us; the launch traced here: 354 us
  waiting for transfers between devices  158 us (45%)
  matrix products  83 us (23%)
  local copies, waits for them, and re-layouts  37.7 us (11%)
  starting transfers between devices  29.3 us (8%)
  loops' own time  23.2 us (7%)
  between operations  13.5 us (4%)
  other arithmetic  8.42 us (2%)
    all_gather x1, waiting for transfers between devices, side_by_side(): result = lax.all_gather(both, axis, axis=dim, tiled=True)  148 us
    dot_general x33, matrix products, absorb(): jnp.einsum('qhd,khd->hqk', query_three, key_three, preferred_element_type...  39.8 us
    dot_general x33, matrix products, absorb(): jnp.einsum('hqk,khd->hqd', weights.astype(jnp.bfloat16), value_three, pre...  39.7 us
    all_to_all x1, starting transfers between devices, on_device(): lax.all_to_all(attended, 'head', split_axis=0, concat_axis=1, tiled=True)  29.3 us
    another operation x1, loops' own time, on_device(): lax.scan(advance, fold_running, jnp.arange(length // tok_blk, dtype=jnp.i...  23.2 us
    dynamic_slice x32, local copies, waits for them, and re-layouts, on_device(): lax.scan(advance, fold_running, jnp.arange(length // tok_blk, dtype=jnp.i...  20.8 us
    all_to_all x1, waiting for transfers between devices, on_device(): lax.all_to_all(attended, 'head', split_axis=0, concat_axis=1, tiled=True)  9.44 us
    split x1, local copies, waits for them, and re-layouts, side_by_side(): jnp.split(result, [sum(widths[:k]) for k in range(1, len(widths))], axis=...  7.34 us
  transfers between devices with their start and end apart: 3, of which 2 were waited for; matrix products, arithmetic and copies ran while one was open for 35% of the time, Pallas kernels for 0%

commit v1 on v0

v1 whole, which is shorter than its diff:
```python
import functools
import math

import jax
import jax.numpy as jnp
from jax import lax
from jax.experimental import pallas as pl
from jax.experimental.pallas import tpu as pltpu
from jax.sharding import PartitionSpec as P

HD = 64
TEXT = 154
BS = 128
TOK = 512
YL = 4
ZL = 8
NH = 16
D = 1536
ROWS = TOK // NH
TSLOTS = 3
FAR = -(2.0**100)
RATE = math.log2(math.e) / math.sqrt(HD)
MESH = pl.DeviceIdType.MESH
BF = jnp.bfloat16
F32 = jnp.float32
NT = (((1,), (1,)), ((), ()))


def flip(index, mask, bits):
    total = 0
    for b in range(bits):
        bit = (index // (1 << b)) % 2
        total = total + (1 << b) * ((1 - bit) if (mask >> b) & 1 else bit)
    return total


def iota(shape, dim):
    return lax.broadcasted_iota(jnp.int32, shape, dim)


def kernel(
    q_ref, k_ref, v_ref, tk_ref, tv_ref, img_ref, gate_ref, res_ref, w_ref,
    out_ref,
    kv, qt, qa, ka, va, acc, mx, tpad, osend, orecv, ssend, srecv, attl, atth, arecv, wbuf,
    q_s, q_r, kv_s, kv_r, w_s, w_r, o_s, o_r, st_s, st_r, a_s, a_r,
):
    blk = lax.axis_index("blk")
    head = lax.axis_index("head")
    z = blk // YL
    y = blk % YL
    zright = ((z + 1) % ZL) * YL + y
    zleft = ((z + ZL - 1) % ZL) * YL + y
    ypeer = [z * YL + flip(y, c, 2) for c in range(YL)]
    hpeer = [flip(head, s, 4) for s in range(NH)]

    barrier = pltpu.get_barrier_semaphore()
    for other in (zright, zleft, ypeer[1], ypeer[2], ypeer[3]):
        pl.semaphore_signal(barrier, inc=1, device_id={"blk": other}, device_id_type=MESH)
    for s in range(1, NH):
        pl.semaphore_signal(barrier, inc=1, device_id={"head": hpeer[s]}, device_id_type=MESH)

    eye = (iota((HD, HD), 0) == iota((HD, HD), 1)).astype(F32).astype(BF)
    low = (iota((HD, 128), 0) == iota((HD, 128), 1)).astype(F32).astype(BF)
    high = (iota((HD, 128), 0) + HD == iota((HD, 128), 1)).astype(F32).astype(BF)

    pack = jnp.dot(k_ref[...], low, preferred_element_type=F32)
    pack = pack + jnp.dot(v_ref[...], high, preferred_element_type=F32)
    kv[0] = pack.astype(BF)
    qt[0] = lax.dot_general(eye, q_ref[...], NT, preferred_element_type=F32).astype(BF)

    pl.semaphore_wait(barrier, 5 + NH - 1)

    started = []

    def send(src, dst, ssem, rsem, dev):
        copy = pltpu.make_async_remote_copy(
            src_ref=src, dst_ref=dst, send_sem=ssem, recv_sem=rsem,
            device_id=dev, device_id_type=MESH,
        )
        copy.start()
        started.append(copy)
        return copy

    def q_copy(c):
        return send(qt.at[0], qt.at[c], q_s.at[c - 1], q_r.at[c - 1], {"blk": ypeer[c]})

    def kv_right(step):
        src = 0 if step == 1 else ZL - (step - 1)
        dst = ZL - step
        rows = pl.ds(0, TOK // 2) if step == 4 else pl.ds(0, TOK)
        return send(kv.at[src, rows], kv.at[dst, rows], kv_s.at[step - 1], kv_r.at[step - 1], {"blk": zright})

    def kv_left(step):
        rows = pl.ds(TOK // 2, TOK // 2) if step == 4 else pl.ds(0, TOK)
        return send(kv.at[step - 1, rows], kv.at[step, rows], kv_s.at[step + 3], kv_r.at[step + 3], {"blk": zleft})

    w_count = [0]

    def w_copy(origin, to):
        src = w_ref if origin == 0 else wbuf.at[pl.ds(origin * HD, HD)]
        slot = origin ^ to
        k = w_count[0]
        w_count[0] += 1
        return send(src, wbuf.at[pl.ds(slot * HD, HD)], w_s.at[k], w_r.at[slot], {"head": hpeer[to]})

    def w_wait(slot):
        part = wbuf.at[pl.ds(slot * HD, HD)]
        pltpu.make_async_remote_copy(
            src_ref=part, dst_ref=part, send_sem=w_s.at[0], recv_sem=w_r.at[slot],
            device_id={"head": hpeer[1]}, device_id_type=MESH,
        ).wait_recv()

    q_cps = [None] + [q_copy(c) for c in (1, 2, 3)]
    r_cps = {1: kv_right(1)}
    l_cps = {1: kv_left(1)}
    w_copy(0, 2)
    for s in (4, 12, 8):
        w_copy(0, s)
    w_copy(0, 1)
    wbuf[pl.ds(0, HD)] = w_ref[...]

    lane = iota((BS, 128), 1)

    def fill_keys(slot, packet, first_block):
        packf = packet.astype(F32)
        for b in range(TOK // BS):
            image = img_ref[first_block + b]
            gap = jnp.where((lane < HD + 8) & (lane != HD + image), FAR, 0.0)
            rows = jnp.where(lane < HD, packf[b * BS : (b + 1) * BS], gap)
            ka[slot, b * BS : (b + 1) * BS] = rows.astype(BF)
        vt = lax.dot_general(high, packet, NT, preferred_element_type=F32)
        va[slot, 0:HD] = vt.astype(BF)
        va[slot, HD : HD + 16] = jnp.ones((16, TOK), BF)

    def fill_queries(c):
        qa[c, 0:HD] = qt[c]
        first = ypeer[c] * (TOK // BS)
        for b in range(TOK // BS):
            image = img_ref[first + b]
            hot = (iota((16, BS), 0) == image).astype(F32)
            qa[c, HD : HD + 16, b * BS : (b + 1) * BS] = hot.astype(BF)
        qa[c, HD + 16 : 128] = jnp.zeros((128 - HD - 16, TOK), BF)

    def process(slot, c):
        keys = ka[slot]
        vals = va[slot]
        for part in range(2):
            cols = slice(part * 256, part * 256 + 256)
            sc = jnp.dot(keys, qa[c, :, cols], preferred_element_type=F32)
            old = mx[c, 0:1, cols]
            new = jnp.maximum(old, jnp.max(sc, axis=0, keepdims=True))
            pr = jnp.exp2((sc - new) * RATE).astype(BF)
            shrink = jnp.exp2((old - new) * RATE)
            upd = jnp.dot(vals, pr, preferred_element_type=F32)
            acc[c, :, cols] = acc[c, :, cols] * shrink + upd
            mx[c, 0:1, cols] = new

    for c in range(YL):
        acc[c] = jnp.zeros((HD + 16, TOK), F32)
        mx[c] = jnp.full((8, TOK), FAR, F32)

    fill_queries(0)
    ntext = tk_ref.shape[0]
    tpad[0, 0:ntext] = tk_ref[...]
    tpad[0, ntext:] = jnp.zeros((TSLOTS * TOK - ntext, HD), BF)
    tpad[1, 0:ntext] = tv_ref[...]
    tpad[1, ntext:] = jnp.zeros((TSLOTS * TOK - ntext, HD), BF)
    for t in range(TSLOTS):
        rows = iota((TOK, 128), 0) + t * TOK
        cols = iota((TOK, 128), 1) - HD
        inside = (rows >= cols * TEXT) & (rows < (cols + 1) * TEXT)
        gap = jnp.where((cols >= 0) & (cols < 8) & jnp.logical_not(inside), FAR, 0.0)
        tk = tpad[0, t * TOK : (t + 1) * TOK]
        tv = tpad[1, t * TOK : (t + 1) * TOK]
        ka[ZL + t] = (jnp.dot(tk, low, preferred_element_type=F32) + gap).astype(BF)
        va[ZL + t, 0:HD] = lax.dot_general(eye, tv, NT, preferred_element_type=F32).astype(BF)
        va[ZL + t, HD : HD + 16] = jnp.ones((16, TOK), BF)

    fill_keys(0, kv[0], blk * (TOK // BS))

    def own_step(t, carry):
        slot = (ZL + t) % (ZL + TSLOTS)
        process(slot, 0)
        return carry

    lax.fori_loop(0, TSLOTS + 1, own_step, 0)

    for c in (1, 2, 3):
        q_cps[c].wait_recv()
        fill_queries(c)

    def first_step(c, carry):
        process(0, c)
        return carry

    lax.fori_loop(1, YL, first_step, 0)

    def origin_block(slot):
        return (((z + slot) % ZL) * YL + y) * (TOK // BS)

    for step in (1, 2, 3):
        r_cps[step].wait_recv()
        r_cps[step + 1] = kv_right(step + 1)
        l_cps[step].wait_recv()
        l_cps[step + 1] = kv_left(step + 1)
        fill_keys(ZL - step, kv[ZL - step], origin_block(ZL - step))
        fill_keys(step, kv[step], origin_block(step))

        def mid_step(t, carry, step=step):
            side = t // YL
            slot = step + side * (ZL - 2 * step)
            process(slot, t % YL)
            return carry

        lax.fori_loop(0, 2 * YL, mid_step, 0)
        if step == 1:
            for s in (4, 12, 8):
                w_wait(s)
                w_copy(s, 1)
        if step == 2:
            w_wait(2)
            for s in (4, 12, 8):
                w_copy(2, s)
            w_copy(2, 1)

    r_cps[4].wait_recv()
    l_cps[4].wait_recv()
    fill_keys(4, kv[4], origin_block(4))
    o_cps = [None] * YL
    st_cps = [None] * YL
    for c in (3, 2, 1):
        process(4, c)
        osend[c - 1] = acc[c, 0:HD].astype(BF)
        ssend[c - 1, 0:1] = mx[c, 0:1]
        ssend[c - 1, 1:2] = acc[c, HD : HD + 1]
        ssend[c - 1, 2:8] = jnp.zeros((6, TOK), F32)
        dev = {"blk": ypeer[c]}
        o_cps[c] = send(osend.at[c - 1], orecv.at[c - 1], o_s.at[c - 1], o_r.at[c - 1], dev)
        st_cps[c] = send(ssend.at[c - 1], srecv.at[c - 1], st_s.at[c - 1], st_r.at[c - 1], dev)
    process(4, 0)
    for s in (6, 14, 10):
        w_wait(s)
        w_copy(s, 1)
    for c in (1, 2, 3):
        o_cps[c].wait_recv()
        st_cps[c].wait_recv()

    maxes = [mx[0, 0:1]] + [srecv[c - 1, 0:1] for c in (1, 2, 3)]
    sums = [acc[0, HD : HD + 1]] + [srecv[c - 1, 1:2] for c in (1, 2, 3)]
    top = functools.reduce(jnp.maximum, maxes)
    scales = [jnp.exp2((m - top) * RATE) for m in maxes]
    denom = functools.reduce(jnp.add, [s * l for s, l in zip(scales, sums)])
    numer = acc[0, 0:HD] * scales[0]
    for c in (1, 2, 3):
        numer = numer + orecv[c - 1].astype(F32) * scales[c]
    att = numer / denom
    both = jnp.concatenate([att, att], axis=0).T
    side = iota((TOK, 128), 1) < HD
    attl[...] = jnp.where(side, both, 0.0).astype(BF)
    atth[...] = jnp.where(side, 0.0, both).astype(BF)

    a_cps = []
    for s in range(1, NH):
        src = atth if s % 2 else attl
        start = pl.multiple_of(hpeer[s] * ROWS, ROWS)
        a_cps.append(
            send(src.at[pl.ds(start, ROWS)], arecv.at[s - 1], a_s.at[s - 1], a_r.at[s - 1], {"head": hpeer[s]})
        )
    for s in (1, 5, 13, 9, 3, 7, 15, 11):
        w_wait(s)
    mine = attl[pl.ds(pl.multiple_of(head * ROWS, ROWS), ROWS)]
    for cp in a_cps:
        cp.wait_recv()
    pairs = [mine + arecv[0]]
    for i in range(1, NH // 2):
        pairs.append(arecv[2 * i - 1] + arecv[2 * i])
    mixed = jnp.concatenate(pairs, axis=1)
    image = img_ref[blk * (TOK // BS) + head // (NH * BS // TOK)]
    gating = gate_ref[pl.ds(image, 1), :]
    projected = jnp.dot(mixed, wbuf[...], preferred_element_type=F32)
    out_ref[...] = (res_ref[...].astype(F32) + gating * projected).astype(BF)
    for cp in started:
        cp.wait_send()


def on_device(queries, key_rows, values, text_keys, text_values, block_image, gate_image, residual, w_out):
    vm = pl.BlockSpec(memory_space=pltpu.VMEM)
    sm = pl.BlockSpec(memory_space=pltpu.SMEM)
    dma = pltpu.SemaphoreType.DMA
    return pl.pallas_call(
        kernel,
        out_shape=jax.ShapeDtypeStruct((ROWS, D), BF),
        in_specs=[vm, vm, vm, vm, vm, sm, vm, vm, vm],
        out_specs=vm,
        scratch_shapes=[
            pltpu.VMEM((ZL, TOK, 128), BF),
            pltpu.VMEM((YL, HD, TOK), BF),
            pltpu.VMEM((YL, 128, TOK), BF),
            pltpu.VMEM((ZL + TSLOTS, TOK, 128), BF),
            pltpu.VMEM((ZL + TSLOTS, HD + 16, TOK), BF),
            pltpu.VMEM((YL, HD + 16, TOK), F32),
            pltpu.VMEM((YL, 8, TOK), F32),
            pltpu.VMEM((2, TSLOTS * TOK, HD), BF),
            pltpu.VMEM((3, HD, TOK), BF),
            pltpu.VMEM((3, HD, TOK), BF),
            pltpu.VMEM((3, 8, TOK), F32),
            pltpu.VMEM((3, 8, TOK), F32),
            pltpu.VMEM((TOK, 128), BF),
            pltpu.VMEM((TOK, 128), BF),
            pltpu.VMEM((NH - 1, ROWS, 128), BF),
            pltpu.VMEM((NH * HD, D), BF),
            dma((3,)), dma((3,)),
            dma((8,)), dma((8,)),
            dma((15,)), dma((16,)),
            dma((3,)), dma((3,)),
            dma((3,)), dma((3,)),
            dma((15,)), dma((15,)),
        ],
        compiler_params=pltpu.CompilerParams(
            collective_id=0, has_side_effects=True, vmem_limit_bytes=48 * 1024 * 1024
        ),
        name="joint_attention",
    )(queries, key_rows, values, text_keys, text_values, block_image, gate_image, residual, w_out)


def solution(mesh):
    placed = (
        P("blk", "head"),
        P("blk", "head"),
        P("blk", "head"),
        P(None, "head"),
        P(None, "head"),
        P(),
        P(),
        P(("blk", "head"), None),
        P("head", None),
    )
    return jax.shard_map(
        on_device, mesh=mesh, in_specs=placed, out_specs=P(("blk", "head"), None), check_vma=False
    )
```

time: 355 us -> 76.3 us (0.21)
  waiting for transfers between devices: 158 us -> 0 us
  matrix products: 83 us -> 0 us
  Pallas kernels: 0 us -> 71.6 us
  local copies, waits for them, and re-layouts: 37.7 us -> 4.43 us
  starting transfers between devices: 29.3 us -> 0 us
  loops' own time: 23.2 us -> 0 us
  between operations: 13.5 us -> 0.06 us
  other arithmetic: 8.42 us -> 0 us
    all_gather x2 -> x0, waiting for transfers between devices: 148 us -> none  [the longest x1 148 us: side_by_side(): result = lax.all_gather(both, axis, axis=dim, tiled=True)]
    dot_general x68 -> x0, matrix products: 83 us -> none  [the longest x33 39.8 us: absorb(): jnp.einsum('qhd,khd->hqk', query_three, key_three, preferred_element_type...]
    pallas_call x0 -> x1, Pallas kernels: none -> 71.6 us  [on_device(): pl.pallas_call(kernel, out_shape=jax.ShapeDtypeStruct((ROWS, D), BF), in_...]
    all_to_all x1 -> x0, starting transfers between devices: 29.3 us -> none  [on_device(): lax.all_to_all(attended, 'head', split_axis=0, concat_axis=1, tiled=True)]
    dynamic_slice x66 -> x0, local copies, waits for them, and re-layouts: 24.1 us -> none  [the longest x32 20.8 us: on_device(): lax.scan(advance, fold_running, jnp.arange(length // tok_blk, dtype=jnp.i...]
    another operation x1 -> x0, loops' own time: 23.2 us -> none  [on_device(): lax.scan(advance, fold_running, jnp.arange(length // tok_blk, dtype=jnp.i...]
    all_to_all x1 -> x0, waiting for transfers between devices: 9.44 us -> none  [on_device(): lax.all_to_all(attended, 'head', split_axis=0, concat_axis=1, tiled=True)]
    split x1 -> x0, local copies, waits for them, and re-layouts: 7.34 us -> none  [side_by_side(): jnp.split(result, [sum(widths[:k]) for k in range(1, len(widths))], axis=...]
  transfers between devices with their start and end apart: 3 -> 0, of which waited for: 2 -> 0; matrix products, arithmetic and copies ran while one was open for 35% -> 0% of each run, Pallas kernels for 0% -> 0%
where the time goes in v1:
time: 76.3 us; the launch traced here: 76.1 us
  Pallas kernels  71.6 us (94%)
  local copies, waits for them, and re-layouts  4.43 us (6%)
    pallas_call x1, Pallas kernels, on_device(): pl.pallas_call(kernel, out_shape=jax.ShapeDtypeStruct((ROWS, D), BF), in_...  71.6 us
    unnamed x22, local copies, waits for them, and re-layouts  4.43 us

profile of v1, /device:TPU:1, one launch (start us, length us, event | category | flops | bytes accessed | tf_op | source)
XLA Modules:
  0.0 76.1 jit_solution(9063971866984930418)
XLA Ops:
  0.0 0.0 copy-start.6
  0.0 0.0 copy-start.7
  0.0 1.0 %copy.10.q_ref = bf16[512,64]{1,0:T(8,128)(2,1)S(1)} copy(bf16[512,64]{0,1:T(8,128)(2,1)} %param.9) | data formatting | bytes 131072 | tf_op args[0]
  1.0 0.0 copy-done.6
  1.0 0.0 copy-start.4
  1.0 0.1 copy.11.k_ref
  1.1 0.0 copy-done.7
  1.2 0.1 copy.12.v_ref
  1.3 0.6 copy-done.4
  1.9 0.0 copy-start.5
  1.9 0.2 copy.13.tk_ref
  2.1 0.7 copy-done.5
  2.8 0.0 copy-start
  2.8 0.0 copy-start.1
  2.9 0.0 copy-start.2
  2.9 0.0 copy-start.3
  2.9 0.2 copy.14.tv_ref
  3.1 0.7 copy-done
  3.8 0.1 copy-done.1
  3.8 0.0 copy-done.2
  3.8 0.0 copy-done.3
  3.8 71.6 %joint_attention.1 = bf16[32,1536]{1,0:T(8,128)(2,1)S(1)} custom-call(bf16[512,64]{1,0:T(8,128)(2,1)S(1)} %copy.10.q_ref, bf16[512,64]{1,0:T(8,128)(2,1)S(1)} %copy.11.k_ref, bf16[512,64]{1,0:T(8,128)(2,1)S(1)} %copy.12.v_ref, bf16[1232,64]{1,0:T(8,128)(2,1)S(1)} %copy.13.tk_ref, bf16[1232,64]{1,0:T(8,128)(2,1)S(1)} %copy.14.tv_ref, s32[128]{0:T(128)S(1)} %copy-done.3, ...), custom_call_target="tpu_custom_call" | custom-call | tf_op jit(solution)/shard_map/joint_attention/pallas_call | solution.py:290
  75.4 0.6 copy.16
Async XLA Ops:
  0.0 1.0 %copy-start.6 = (bf16[512,64]{0,1:T(8,128)(2,1)S(1)}, bf16[512,64]{0,1:T(8,128)(2,1)}, u32[]{:S(2)}) copy-start(bf16[512,64]{0,1:T(8,128)(2,1)} %param.10) | copy-start | bytes 196612
  0.0 1.1 %copy-start.7 = (bf16[512,64]{0,1:T(8,128)(2,1)S(1)}, bf16[512,64]{0,1:T(8,128)(2,1)}, u32[]{:S(2)}) copy-start(bf16[512,64]{0,1:T(8,128)(2,1)} %param.11) | copy-start | bytes 196612
  1.0 0.9 %copy-start.4 = (bf16[1232,64]{0,1:T(8,128)(2,1)S(1)}, bf16[1232,64]{0,1:T(8,128)(2,1)}, u32[]{:S(2)}) copy-start(bf16[1232,64]{0,1:T(8,128)(2,1)} %param.12) | copy-start | bytes 473092
  1.9 0.9 %copy-start.5 = (bf16[1232,64]{0,1:T(8,128)(2,1)S(1)}, bf16[1232,64]{0,1:T(8,128)(2,1)}, u32[]{:S(2)}) copy-start(bf16[1232,64]{0,1:T(8,128)(2,1)} %param.13) | copy-start | bytes 473092
  2.8 0.9 %copy-start = (bf16[64,1536]{1,0:T(8,128)(2,1)S(1)}, bf16[64,1536]{1,0:T(8,128)(2,1)}, u32[]{:S(2)}) copy-start(bf16[64,1536]{1,0:T(8,128)(2,1)} %w_ref.1) | copy-start | bytes 589828
  2.8 1.0 %copy-start.1 = (bf16[32,1536]{1,0:T(8,128)(2,1)S(1)}, bf16[32,1536]{1,0:T(8,128)(2,1)}, u32[]{:S(2)}) copy-start(bf16[32,1536]{1,0:T(8,128)(2,1)} %res_ref.1) | copy-start | bytes 294916
  2.9 1.0 %copy-start.2 = (f32[8,1536]{1,0:T(8,128)S(1)}, f32[8,1536]{1,0:T(8,128)}, u32[]{:S(2)}) copy-start(f32[8,1536]{1,0:T(8,128)} %gate_ref.1) | copy-start | bytes 147460
  2.9 1.0 %copy-start.3 = (s32[128]{0:T(128)S(1)}, s32[128]{0:T(128)}, u32[]{:S(2)}) copy-start(s32[128]{0:T(128)} %img_ref.1) | copy-start | bytes 1540

commit v2 on v1

--- a/solution.py
+++ b/solution.py
@@ -39,10 +39,10 @@
 
 
 def kernel(
-    q_ref, k_ref, v_ref, tk_ref, tv_ref, img_ref, gate_ref, res_ref, w_ref,
+    q_hbm, k_hbm, v_hbm, tk_hbm, tv_hbm, img_ref, gate_hbm, res_hbm, w_hbm,
     out_ref,
-    kv, qt, qa, ka, va, acc, mx, tpad, osend, orecv, ssend, srecv, attl, atth, arecv, wbuf,
-    q_s, q_r, kv_s, kv_r, w_s, w_r, o_s, o_r, st_s, st_r, a_s, a_r,
+    kv, qt, tk_ref, tv_ref, gate_ref, res_ref, qa, ka, va, acc, mx, tpad, osend, orecv, ssend, srecv, attl, atth, arecv, wbuf,
+    q_s, q_r, kv_s, kv_r, w_s, w_r, o_s, o_r, st_s, st_r, a_s, a_r, in_s,
 ):
     blk = lax.axis_index("blk")
     head = lax.axis_index("head")
@@ -59,16 +59,26 @@
     for s in range(1, NH):
         pl.semaphore_signal(barrier, inc=1, device_id={"head": hpeer[s]}, device_id_type=MESH)
 
-    eye = (iota((HD, HD), 0) == iota((HD, HD), 1)).astype(F32).astype(BF)
-    low = (iota((HD, 128), 0) == iota((HD, 128), 1)).astype(F32).astype(BF)
-    high = (iota((HD, 128), 0) + HD == iota((HD, 128), 1)).astype(F32).astype(BF)
-
-    pack = jnp.dot(k_ref[...], low, preferred_element_type=F32)
-    pack = pack + jnp.dot(v_ref[...], high, preferred_element_type=F32)
-    kv[0] = pack.astype(BF)
-    qt[0] = lax.dot_general(eye, q_ref[...], NT, preferred_element_type=F32).astype(BF)
-
-    pl.semaphore_wait(barrier, 5 + NH - 1)
+    loads = [
+        pltpu.make_async_copy(src, dst, in_s.at[n])
+        for n, (src, dst) in enumerate((
+            (q_hbm, qt.at[0]),
+            (k_hbm, kv.at[0, pl.ds(0, HD)]),
+            (v_hbm, kv.at[0, pl.ds(HD, HD)]),
+            (w_hbm, wbuf.at[pl.ds(0, HD)]),
+            (tk_hbm, tk_ref),
+            (tv_hbm, tv_ref),
+            (gate_hbm, gate_ref),
+            (res_hbm, res_ref),
+        ))
+    ]
+    for cp in loads:
+        cp.start()
+
+    for cp in loads[:4]:
+        cp.wait()
+    with jax.named_scope("barrier"):
+        pl.semaphore_wait(barrier, 5 + NH - 1)
 
     started = []
 
@@ -87,17 +97,17 @@
     def kv_right(step):
         src = 0 if step == 1 else ZL - (step - 1)
         dst = ZL - step
-        rows = pl.ds(0, TOK // 2) if step == 4 else pl.ds(0, TOK)
+        rows = pl.ds(0, HD) if step == 4 else pl.ds(0, 2 * HD)
         return send(kv.at[src, rows], kv.at[dst, rows], kv_s.at[step - 1], kv_r.at[step - 1], {"blk": zright})
 
     def kv_left(step):
-        rows = pl.ds(TOK // 2, TOK // 2) if step == 4 else pl.ds(0, TOK)
+        rows = pl.ds(HD, HD) if step == 4 else pl.ds(0, 2 * HD)
         return send(kv.at[step - 1, rows], kv.at[step, rows], kv_s.at[step + 3], kv_r.at[step + 3], {"blk": zleft})
 
     w_count = [0]
 
     def w_copy(origin, to):
-        src = w_ref if origin == 0 else wbuf.at[pl.ds(origin * HD, HD)]
+        src = wbuf.at[pl.ds(origin * HD, HD)]
         slot = origin ^ to
         k = w_count[0]
         w_count[0] += 1
@@ -117,19 +127,16 @@
     for s in (4, 12, 8):
         w_copy(0, s)
     w_copy(0, 1)
-    wbuf[pl.ds(0, HD)] = w_ref[...]
-
-    lane = iota((BS, 128), 1)
-
-    def fill_keys(slot, packet, first_block):
-        packf = packet.astype(F32)
+
+    def fill_keys(slot, first_block):
+        row = iota((HD, BS), 0)
+        gaps = []
         for b in range(TOK // BS):
             image = img_ref[first_block + b]
-            gap = jnp.where((lane < HD + 8) & (lane != HD + image), FAR, 0.0)
-            rows = jnp.where(lane < HD, packf[b * BS : (b + 1) * BS], gap)
-            ka[slot, b * BS : (b + 1) * BS] = rows.astype(BF)
-        vt = lax.dot_general(high, packet, NT, preferred_element_type=F32)
-        va[slot, 0:HD] = vt.astype(BF)
+            gaps.append(jnp.where((row < 8) & (row != image), FAR, 0.0))
+        wide = jnp.concatenate([kv[slot, 0:HD].astype(F32), jnp.concatenate(gaps, axis=1)], axis=0)
+        ka[slot] = wide.T.astype(BF)
+        va[slot, 0:HD] = kv[slot, HD : 2 * HD]
         va[slot, HD : HD + 16] = jnp.ones((16, TOK), BF)
 
     def fill_queries(c):
@@ -160,33 +167,38 @@
         mx[c] = jnp.full((8, TOK), FAR, F32)
 
     fill_queries(0)
-    ntext = tk_ref.shape[0]
-    tpad[0, 0:ntext] = tk_ref[...]
-    tpad[0, ntext:] = jnp.zeros((TSLOTS * TOK - ntext, HD), BF)
-    tpad[1, 0:ntext] = tv_ref[...]
-    tpad[1, ntext:] = jnp.zeros((TSLOTS * TOK - ntext, HD), BF)
+    loads[4].wait()
+    loads[5].wait()
+    ntext = tk_ref.shape[1]
+    edge = (TSLOTS - 1) * TOK
+    for n, ref in ((0, tk_ref), (1, tv_ref)):
+        tpad[n, :, edge:] = jnp.zeros((HD, TOK), BF)
+        tpad[n, :, 0:ntext] = ref[...]
     for t in range(TSLOTS):
-        rows = iota((TOK, 128), 0) + t * TOK
-        cols = iota((TOK, 128), 1) - HD
-        inside = (rows >= cols * TEXT) & (rows < (cols + 1) * TEXT)
-        gap = jnp.where((cols >= 0) & (cols < 8) & jnp.logical_not(inside), FAR, 0.0)
-        tk = tpad[0, t * TOK : (t + 1) * TOK]
-        tv = tpad[1, t * TOK : (t + 1) * TOK]
-        ka[ZL + t] = (jnp.dot(tk, low, preferred_element_type=F32) + gap).astype(BF)
-        va[ZL + t, 0:HD] = lax.dot_general(eye, tv, NT, preferred_element_type=F32).astype(BF)
+        row = iota((HD, TOK), 0)
+        col = iota((HD, TOK), 1) + t * TOK
+        inside = (col >= row * TEXT) & (col < (row + 1) * TEXT)
+        gap = jnp.where((row < 8) & jnp.logical_not(inside), FAR, 0.0)
+        span = slice(t * TOK, (t + 1) * TOK)
+        wide = jnp.concatenate([tpad[0, :, span].astype(F32), gap], axis=0)
+        ka[ZL + t] = wide.T.astype(BF)
+        va[ZL + t, 0:HD] = tpad[1, :, span]
         va[ZL + t, HD : HD + 16] = jnp.ones((16, TOK), BF)
 
-    fill_keys(0, kv[0], blk * (TOK // BS))
+    fill_keys(0, blk * (TOK // BS))
 
     def own_step(t, carry):
         slot = (ZL + t) % (ZL + TSLOTS)
         process(slot, 0)
         return carry
 
-    lax.fori_loop(0, TSLOTS + 1, own_step, 0)
-
+    with jax.named_scope("own"):
+        lax.fori_loop(0, TSLOTS + 1, own_step, 0)
+
+    with jax.named_scope("qwait"):
+        for c in (1, 2, 3):
+            q_cps[c].wait_recv()
     for c in (1, 2, 3):
-        q_cps[c].wait_recv()
         fill_queries(c)
 
     def first_step(c, carry):
@@ -199,12 +211,13 @@
         return (((z + slot) % ZL) * YL + y) * (TOK // BS)
 
     for step in (1, 2, 3):
-        r_cps[step].wait_recv()
-        r_cps[step + 1] = kv_right(step + 1)
-        l_cps[step].wait_recv()
-        l_cps[step + 1] = kv_left(step + 1)
-        fill_keys(ZL - step, kv[ZL - step], origin_block(ZL - step))
-        fill_keys(step, kv[step], origin_block(step))
+        with jax.named_scope(f"kvwait{step}"):
+            r_cps[step].wait_recv()
+            r_cps[step + 1] = kv_right(step + 1)
+            l_cps[step].wait_recv()
+            l_cps[step + 1] = kv_left(step + 1)
+        fill_keys(ZL - step, origin_block(ZL - step))
+        fill_keys(step, origin_block(step))
 
         def mid_step(t, carry, step=step):
             side = t // YL
@@ -215,17 +228,20 @@
         lax.fori_loop(0, 2 * YL, mid_step, 0)
         if step == 1:
             for s in (4, 12, 8):
-                w_wait(s)
+                with jax.named_scope("wxwait"):
+                    w_wait(s)
                 w_copy(s, 1)
         if step == 2:
-            w_wait(2)
+            with jax.named_scope("wywait"):
+                w_wait(2)
             for s in (4, 12, 8):
                 w_copy(2, s)
             w_copy(2, 1)
 
-    r_cps[4].wait_recv()
-    l_cps[4].wait_recv()
-    fill_keys(4, kv[4], origin_block(4))
+    with jax.named_scope("kvwait4"):
+        r_cps[4].wait_recv()
+        l_cps[4].wait_recv()
+    fill_keys(4, origin_block(4))
     o_cps = [None] * YL
     st_cps = [None] * YL
     for c in (3, 2, 1):
@@ -239,11 +255,13 @@
         st_cps[c] = send(ssend.at[c - 1], srecv.at[c - 1], st_s.at[c - 1], st_r.at[c - 1], dev)
     process(4, 0)
     for s in (6, 14, 10):
-        w_wait(s)
+        with jax.named_scope("wxwait2"):
+            w_wait(s)
         w_copy(s, 1)
-    for c in (1, 2, 3):
-        o_cps[c].wait_recv()
-        st_cps[c].wait_recv()
+    with jax.named_scope("owait"):
+        for c in (1, 2, 3):
+            o_cps[c].wait_recv()
+            st_cps[c].wait_recv()
 
     maxes = [mx[0, 0:1]] + [srecv[c - 1, 0:1] for c in (1, 2, 3)]
     sums = [acc[0, HD : HD + 1]] + [srecv[c - 1, 1:2] for c in (1, 2, 3)]
@@ -266,11 +284,15 @@
         a_cps.append(
             send(src.at[pl.ds(start, ROWS)], arecv.at[s - 1], a_s.at[s - 1], a_r.at[s - 1], {"head": hpeer[s]})
         )
-    for s in (1, 5, 13, 9, 3, 7, 15, 11):
-        w_wait(s)
+    with jax.named_scope("wcwait"):
+        for s in (1, 5, 13, 9, 3, 7, 15, 11):
+            w_wait(s)
     mine = attl[pl.ds(pl.multiple_of(head * ROWS, ROWS), ROWS)]
-    for cp in a_cps:
-        cp.wait_recv()
+    with jax.named_scope("await"):
+        for cp in a_cps:
+            cp.wait_recv()
+    loads[6].wait()
+    loads[7].wait()
     pairs = [mine + arecv[0]]
     for i in range(1, NH // 2):
         pairs.append(arecv[2 * i - 1] + arecv[2 * i])
@@ -279,28 +301,34 @@
     gating = gate_ref[pl.ds(image, 1), :]
     projected = jnp.dot(mixed, wbuf[...], preferred_element_type=F32)
     out_ref[...] = (res_ref[...].astype(F32) + gating * projected).astype(BF)
-    for cp in started:
-        cp.wait_send()
+    with jax.named_scope("sendwait"):
+        for cp in started:
+            cp.wait_send()
 
 
 def on_device(queries, key_rows, values, text_keys, text_values, block_image, gate_image, residual, w_out):
     vm = pl.BlockSpec(memory_space=pltpu.VMEM)
+    hb = pl.BlockSpec(memory_space=pl.ANY)
     sm = pl.BlockSpec(memory_space=pltpu.SMEM)
     dma = pltpu.SemaphoreType.DMA
     return pl.pallas_call(
         kernel,
         out_shape=jax.ShapeDtypeStruct((ROWS, D), BF),
-        in_specs=[vm, vm, vm, vm, vm, sm, vm, vm, vm],
+        in_specs=[hb, hb, hb, hb, hb, sm, hb, hb, hb],
         out_specs=vm,
         scratch_shapes=[
-            pltpu.VMEM((ZL, TOK, 128), BF),
+            pltpu.VMEM((ZL, 2 * HD, TOK), BF),
             pltpu.VMEM((YL, HD, TOK), BF),
+            pltpu.VMEM((HD, text_keys.shape[0]), BF),
+            pltpu.VMEM((HD, text_keys.shape[0]), BF),
+            pltpu.VMEM(gate_image.shape, F32),
+            pltpu.VMEM((ROWS, D), BF),
             pltpu.VMEM((YL, 128, TOK), BF),
             pltpu.VMEM((ZL + TSLOTS, TOK, 128), BF),
             pltpu.VMEM((ZL + TSLOTS, HD + 16, TOK), BF),
             pltpu.VMEM((YL, HD + 16, TOK), F32),
             pltpu.VMEM((YL, 8, TOK), F32),
-            pltpu.VMEM((2, TSLOTS * TOK, HD), BF),
+            pltpu.VMEM((2, HD, TSLOTS * TOK), BF),
             pltpu.VMEM((3, HD, TOK), BF),
             pltpu.VMEM((3, HD, TOK), BF),
             pltpu.VMEM((3, 8, TOK), F32),
@@ -315,12 +343,16 @@
             dma((3,)), dma((3,)),
             dma((3,)), dma((3,)),
             dma((15,)), dma((15,)),
+            dma((8,)),
         ],
         compiler_params=pltpu.CompilerParams(
-            collective_id=0, has_side_effects=True, vmem_limit_bytes=48 * 1024 * 1024
+            collective_id=0, has_side_effects=True, vmem_limit_bytes=60 * 1024 * 1024
         ),
         name="joint_attention",
-    )(queries, key_rows, values, text_keys, text_values, block_image, gate_image, residual, w_out)
+    )(
+        queries.T, key_rows.T, values.T, text_keys.T, text_values.T,
+        block_image, gate_image, residual, w_out,
+    )
 
 
 def solution(mesh):

time: 76.3 us -> 73.9 us (0.969)
  local copies, waits for them, and re-layouts: 4.43 us -> 1.54 us
    unnamed x22 -> x1, local copies, waits for them, and re-layouts: 4.43 us -> 1.54 us
where the time goes in v2:
time: 73.9 us; the launch traced here: 73.7 us
  Pallas kernels  72.2 us (98%)
  local copies, waits for them, and re-layouts  1.54 us (2%)
    pallas_call x1, Pallas kernels, on_device(): pl.pallas_call(kernel, out_shape=jax.ShapeDtypeStruct((ROWS, D), BF), in_...  72.2 us
    unnamed x1, local copies, waits for them, and re-layouts  1.54 us

profile of v2, /device:TPU:1, one launch (start us, length us, event | category | flops | bytes accessed | tf_op | source)
XLA Modules:
  0.0 73.7 jit_solution(3444187851500493649)
XLA Ops:
  0.0 72.2 %joint_attention.1 = bf16[32,1536]{1,0:T(8,128)(2,1)} custom-call(bf16[64,512]{1,0:T(8,128)(2,1)} %bitcast.7, bf16[64,512]{1,0:T(8,128)(2,1)} %bitcast.8, bf16[64,512]{1,0:T(8,128)(2,1)} %bitcast.9, bf16[64,1232]{1,0:T(8,128)(2,1)} %bitcast.5, bf16[64,1232]{1,0:T(8,128)(2,1)} %bitcast.6, s32[128]{0:T(128)} %img_ref.1, f32[8,1536]{1,0:T(8,128)} %gate_hbm.1, ...), custom_call_target="tpu_custom_call" | custom-call | tf_op jit(solution)/shard_map/joint_attention/pallas_call | solution.py:314
  72.2 1.5 %copy.11 = bf16[32,1536]{1,0:T(8,128)(2,1)} copy(bf16[32,1536]{1,0:T(8,128)(2,1)} %joint_attention.1) | data formatting | bytes 196608

commit v3 on v2

v3 whole, which is shorter than its diff:
```python
import functools
import math

import jax
import jax.numpy as jnp
from jax import lax
from jax.experimental import pallas as pl
from jax.experimental.pallas import tpu as pltpu
from jax.sharding import PartitionSpec as P

HD = 64
TEXT = 154
BS = 128
TOK = 512
YL = 4
ZL = 8
NH = 16
D = 1536
ROWS = TOK // NH
TSLOTS = 3
FAR = -(2.0**100)
RATE = math.log2(math.e) / math.sqrt(HD)
MESH = pl.DeviceIdType.MESH
BF = jnp.bfloat16
F32 = jnp.float32
NT = (((1,), (1,)), ((), ()))


def flip(index, mask, bits):
    total = 0
    for b in range(bits):
        bit = (index // (1 << b)) % 2
        total = total + (1 << b) * ((1 - bit) if (mask >> b) & 1 else bit)
    return total


def iota(shape, dim):
    return lax.broadcasted_iota(jnp.int32, shape, dim)


def kernel(
    q_hbm, k_hbm, v_hbm, tk_hbm, tv_hbm, img_hbm, gate_hbm, res_hbm, w_hbm,
    out_ref,
    img_ref, kv, qt, tk_ref, tv_ref, gate_ref, res_ref, qa, ka, va, acc, mx, tpad, s0, s1, osend, orecv, ssend, srecv, attl, atth, arecv, wbuf,
    q_s, q_r, kv_s, kv_r, w_s, w_r, o_s, o_r, st_s, st_r, a_s, a_r, in_s,
):
    blk = lax.axis_index("blk")
    head = lax.axis_index("head")
    z = blk // YL
    y = blk % YL
    zright = ((z + 1) % ZL) * YL + y
    zleft = ((z + ZL - 1) % ZL) * YL + y
    ypeer = [z * YL + flip(y, c, 2) for c in range(YL)]
    hpeer = [flip(head, s, 4) for s in range(NH)]

    barrier = pltpu.get_barrier_semaphore()
    for other in (zright, zleft, ypeer[1], ypeer[2], ypeer[3]):
        pl.semaphore_signal(barrier, inc=1, device_id={"blk": other}, device_id_type=MESH)
    for s in range(1, NH):
        pl.semaphore_signal(barrier, inc=1, device_id={"head": hpeer[s]}, device_id_type=MESH)

    loads = [
        pltpu.make_async_copy(src, dst, in_s.at[n])
        for n, (src, dst) in enumerate((
            (img_hbm, img_ref),
            (q_hbm, qt.at[0]),
            (k_hbm, kv.at[0, pl.ds(0, HD)]),
            (v_hbm, kv.at[0, pl.ds(HD, HD)]),
            (w_hbm, wbuf.at[pl.ds(0, HD)]),
            (tk_hbm, tk_ref),
            (tv_hbm, tv_ref),
            (gate_hbm, gate_ref),
            (res_hbm, res_ref),
        ))
    ]
    for cp in loads:
        cp.start()

    started = []

    def send(src, dst, ssem, rsem, dev):
        copy = pltpu.make_async_remote_copy(
            src_ref=src, dst_ref=dst, send_sem=ssem, recv_sem=rsem,
            device_id=dev, device_id_type=MESH,
        )
        copy.start()
        started.append(copy)
        return copy

    def q_copy(c):
        return send(qt.at[0], qt.at[c], q_s.at[c - 1], q_r.at[c - 1], {"blk": ypeer[c]})

    kv_cps = {}

    def kv_send(kind, step):
        src = step - 1 if kind in ("lk", "lv") or step == 1 else ZL - (step - 1)
        dst = step if kind in ("lk", "lv") else ZL - step
        k = {"rk": 0, "rv": 4, "lk": 7, "lv": 10}[kind] + step - 1
        rows = pl.ds(0 if kind in ("rk", "lk") else HD, HD)
        dev = {"blk": zleft if kind in ("lk", "lv") else zright}
        kv_cps[kind, step] = send(kv.at[src, rows], kv.at[dst, rows], kv_s.at[k], kv_r.at[k], dev)

    def kv_hop(step):
        for kind, last in (("rk", 4), ("lk", 3), ("rv", 3), ("lv", 4)):
            if (kind, step) in kv_cps:
                kv_cps[kind, step].wait_recv()
                if step < last:
                    kv_send(kind, step + 1)

    w_count = [0]

    def w_part(slot, half):
        if half is None:
            return wbuf.at[pl.ds(slot * HD, HD)]
        return wbuf.at[pl.ds(slot * HD + half * (HD // 2), HD // 2)]

    def w_sem(slot, half):
        return w_r.at[slot if half in (None, 0) else NH + slot]

    def w_copy(origin, to, half=None):
        slot = origin ^ to
        k = w_count[0]
        w_count[0] += 1
        return send(w_part(origin, half), w_part(slot, half), w_s.at[k], w_sem(slot, half), {"head": hpeer[to]})

    def w_wait(slot, half=None):
        part = w_part(slot, half)
        pltpu.make_async_remote_copy(
            src_ref=part, dst_ref=part, send_sem=w_s.at[0], recv_sem=w_sem(slot, half),
            device_id={"head": hpeer[1]}, device_id_type=MESH,
        ).wait_recv()

    def fill_keys(slot, first_block):
        row = iota((HD, BS), 0)
        gaps = []
        for b in range(TOK // BS):
            image = img_ref[first_block + b]
            gaps.append(jnp.where((row < 8) & (row != image), FAR, 0.0))
        wide = jnp.concatenate([kv[slot, 0:HD].astype(F32), jnp.concatenate(gaps, axis=1)], axis=0)
        ka[slot] = wide.T.astype(BF)
        va[slot, 0:HD] = kv[slot, HD : 2 * HD]
        va[slot, HD : HD + 16] = jnp.ones((16, TOK), BF)

    def fill_queries(c):
        qa[c, 0:HD] = qt[c]
        first = ypeer[c] * (TOK // BS)
        for b in range(TOK // BS):
            image = img_ref[first + b]
            hot = (iota((16, BS), 0) == image).astype(F32)
            qa[c, HD : HD + 16, b * BS : (b + 1) * BS] = hot.astype(BF)
        qa[c, HD + 16 : 128] = jnp.zeros((128 - HD - 16, TOK), BF)

    seen = set()
    pending = []
    turn = [0]

    def scores(slot, c, n, buf):
        sc = jnp.dot(ka[slot, 0:n], qa[c], preferred_element_type=F32)
        buf[0:n] = sc
        buf[TOK : TOK + 8] = jnp.max(sc.reshape(n // 8, 8, TOK), axis=0)

    def soften(slot, c, n, buf):
        new = jnp.max(buf[TOK : TOK + 8], axis=0, keepdims=True)
        if c in seen:
            old = mx[c, 0:1]
            new = jnp.maximum(old, new)
            shrink = jnp.exp2((old - new) * RATE)
        pr = jnp.exp2((buf[0:n] - new) * RATE).astype(BF)
        upd = jnp.dot(va[slot, :, 0:n], pr, preferred_element_type=F32)
        if c in seen:
            acc[c] = acc[c] * shrink + upd
        else:
            acc[c] = upd
        mx[c, 0:1] = new
        seen.add(c)

    def flush():
        while pending:
            soften(*pending.pop(0))

    def steps(*pairs):
        for slot, c in pairs:
            n = tail if slot == ZL + TSLOTS - 1 else TOK
            buf = (s0, s1)[turn[0] % 2]
            turn[0] += 1
            scores(slot, c, n, buf)
            flush()
            pending.append((slot, c, n, buf))

    def origin_block(slot):
        return (((z + slot) % ZL) * YL + y) * (TOK // BS)

    o_cps = [None] * YL
    st_cps = [None] * YL

    def send_part(c):
        osend[c - 1] = acc[c, 0:HD].astype(BF)
        for a in range(4):
            ssend[c - 1, a : a + 1] = mx[c, 0:1, a * 128 : (a + 1) * 128]
            ssend[c - 1, 4 + a : 5 + a] = acc[c, HD : HD + 1, a * 128 : (a + 1) * 128]
        dev = {"blk": ypeer[c]}
        o_cps[c] = send(osend.at[c - 1], orecv.at[c - 1], o_s.at[c - 1], o_r.at[c - 1], dev)
        st_cps[c] = send(ssend.at[c - 1], srecv.at[c - 1], st_s.at[c - 1], st_r.at[c - 1], dev)

    ntext = tk_hbm.shape[1]
    edge = (TSLOTS - 1) * TOK
    tail = -(-(ntext - edge) // 128) * 128
    for cp in loads[:4]:
        cp.wait()
    fill_queries(0)
    fill_keys(0, blk * (TOK // BS))

    with jax.named_scope("barrier"):
        pl.semaphore_wait(barrier, 5 + NH - 1)

    q_cps = [None] + [q_copy(c) for c in (1, 2, 3)]
    for kind in ("rk", "lk", "rv", "lv"):
        kv_send(kind, 1)
    loads[4].wait()
    for s in (4, 12, 8):
        w_copy(0, s)
    w_copy(0, 1)

    loads[5].wait()
    loads[6].wait()
    for n, ref in ((0, tk_ref), (1, tv_ref)):
        tpad[n, :, edge:] = jnp.zeros((HD, TOK), BF)
        tpad[n, :, 0:ntext] = ref[...]
    for t in range(TSLOTS):
        row = iota((HD, TOK), 0)
        col = iota((HD, TOK), 1) + t * TOK
        inside = (col >= row * TEXT) & (col < (row + 1) * TEXT)
        gap = jnp.where((row < 8) & jnp.logical_not(inside), FAR, 0.0)
        span = slice(t * TOK, (t + 1) * TOK)
        wide = jnp.concatenate([tpad[0, :, span].astype(F32), gap], axis=0)
        ka[ZL + t] = wide.T.astype(BF)
        va[ZL + t, 0:HD] = tpad[1, :, span]
        va[ZL + t, HD : HD + 16] = jnp.ones((16, TOK), BF)

    with jax.named_scope("text"):
        steps((8, 0), (9, 0), (10, 0), (0, 0))
        flush()
    with jax.named_scope("qwait1"):
        q_cps[1].wait_recv()
    fill_queries(1)
    steps((0, 1))
    flush()
    with jax.named_scope("kvwait1"):
        kv_hop(1)
    w_copy(0, 2, 0)
    fill_keys(7, origin_block(7))
    fill_keys(1, origin_block(1))
    steps((7, 0), (1, 0), (7, 1), (1, 1))
    flush()
    with jax.named_scope("qwait2"):
        q_cps[2].wait_recv()
    w_copy(0, 2, 1)
    fill_queries(2)
    steps((0, 2), (7, 2), (1, 2))
    flush()
    with jax.named_scope("kvwait2"):
        kv_hop(2)
    fill_keys(6, origin_block(6))
    fill_keys(2, origin_block(2))
    steps((6, 0), (2, 0), (6, 1), (2, 1), (6, 2), (2, 2))
    flush()
    with jax.named_scope("qwait3"):
        q_cps[3].wait_recv()
    fill_queries(3)
    steps((0, 3), (7, 3), (1, 3))
    flush()
    with jax.named_scope("kvwait3"):
        kv_hop(3)
    fill_keys(5, origin_block(5))
    fill_keys(3, origin_block(3))
    steps((6, 3), (2, 3), (5, 0), (3, 0))
    flush()
    with jax.named_scope("wywait"):
        w_wait(2, 0)
    for s in (4, 12, 8):
        w_copy(2, s, 0)
    for s in (4, 12, 8):
        w_wait(s)
        w_copy(s, 1)
    with jax.named_scope("kvwait4"):
        kv_hop(4)
    fill_keys(4, origin_block(4))
    with jax.named_scope("last"):
        steps((5, 3), (3, 3), (4, 3), (5, 2))
        send_part(3)
        steps((3, 2), (4, 2), (5, 1))
        send_part(2)
        steps((3, 1), (4, 1), (4, 0))
        send_part(1)
        flush()
    with jax.named_scope("wywait2"):
        w_wait(2, 1)
    for s in (4, 12, 8):
        w_copy(2, s, 1)
    w_copy(2, 1)
    with jax.named_scope("owait"):
        for c in (1, 2, 3):
            o_cps[c].wait_recv()
            st_cps[c].wait_recv()

    def row_of(ref, c, first):
        return jnp.concatenate([ref[c - 1, first + a : first + a + 1] for a in range(4)], axis=1)

    maxes = [mx[0, 0:1]] + [row_of(srecv, c, 0) for c in (1, 2, 3)]
    sums = [acc[0, HD : HD + 1]] + [row_of(srecv, c, 4) for c in (1, 2, 3)]
    top = functools.reduce(jnp.maximum, maxes)
    scales = [jnp.exp2((m - top) * RATE) for m in maxes]
    denom = functools.reduce(jnp.add, [s * l for s, l in zip(scales, sums)])
    numer = acc[0, 0:HD] * scales[0]
    for c in (1, 2, 3):
        numer = numer + orecv[c - 1].astype(F32) * scales[c]
    att = numer / denom
    both = jnp.concatenate([att, att], axis=0).T
    side = iota((TOK, 128), 1) < HD
    attl[...] = jnp.where(side, both, 0.0).astype(BF)
    atth[...] = jnp.where(side, 0.0, both).astype(BF)

    a_cps = []
    for s in range(1, NH):
        src = atth if s % 2 else attl
        start = pl.multiple_of(hpeer[s] * ROWS, ROWS)
        a_cps.append(
            send(src.at[pl.ds(start, ROWS)], arecv.at[s - 1], a_s.at[s - 1], a_r.at[s - 1], {"head": hpeer[s]})
        )
    for s in (6, 14, 10):
        with jax.named_scope("wxwait2"):
            w_wait(s, 0)
            w_wait(s, 1)
        w_copy(s, 1)
    mine = attl[pl.ds(pl.multiple_of(head * ROWS, ROWS), ROWS)]
    with jax.named_scope("await"):
        for cp in a_cps:
            cp.wait_recv()
    loads[7].wait()
    loads[8].wait()
    with jax.named_scope("wcwait"):
        for s in (1, 5, 13, 9, 3, 7, 15, 11):
            w_wait(s)
    pairs = [mine + arecv[0]]
    for i in range(1, NH // 2):
        pairs.append(arecv[2 * i - 1] + arecv[2 * i])
    mixed = jnp.concatenate(pairs, axis=1)
    image = img_ref[blk * (TOK // BS) + head // (NH * BS // TOK)]
    gating = gate_ref[pl.ds(image, 1), :]
    projected = jnp.dot(mixed, wbuf[...], preferred_element_type=F32)
    out_ref[...] = (res_ref[...].astype(F32) + gating * projected).astype(BF)
    with jax.named_scope("sendwait"):
        for cp in started:
            cp.wait_send()


def on_device(queries, key_rows, values, text_keys, text_values, block_image, gate_image, residual, w_out):
    vm = pl.BlockSpec(memory_space=pltpu.VMEM)
    hb = pl.BlockSpec(memory_space=pl.ANY)
    dma = pltpu.SemaphoreType.DMA
    return pl.pallas_call(
        kernel,
        out_shape=jax.ShapeDtypeStruct((ROWS, D), BF),
        in_specs=[hb] * 9,
        out_specs=vm,
        scratch_shapes=[
            pltpu.SMEM(block_image.shape, jnp.int32),
            pltpu.VMEM((ZL, 2 * HD, TOK), BF),
            pltpu.VMEM((YL, HD, TOK), BF),
            pltpu.VMEM((HD, text_keys.shape[0]), BF),
            pltpu.VMEM((HD, text_keys.shape[0]), BF),
            pltpu.VMEM(gate_image.shape, F32),
            pltpu.VMEM((ROWS, D), BF),
            pltpu.VMEM((YL, 128, TOK), BF),
            pltpu.VMEM((ZL + TSLOTS, TOK, 128), BF),
            pltpu.VMEM((ZL + TSLOTS, HD + 16, TOK), BF),
            pltpu.VMEM((YL, HD + 16, TOK), F32),
            pltpu.VMEM((YL, 8, TOK), F32),
            pltpu.VMEM((2, HD, TSLOTS * TOK), BF),
            pltpu.VMEM((TOK + 8, TOK), F32),
            pltpu.VMEM((TOK + 8, TOK), F32),
            pltpu.VMEM((3, HD, TOK), BF),
            pltpu.VMEM((3, HD, TOK), BF),
            pltpu.VMEM((3, 8, 128), F32),
            pltpu.VMEM((3, 8, 128), F32),
            pltpu.VMEM((TOK, 128), BF),
            pltpu.VMEM((TOK, 128), BF),
            pltpu.VMEM((NH - 1, ROWS, 128), BF),
            pltpu.VMEM((NH * HD, D), BF),
            dma((3,)), dma((3,)),
            dma((14,)), dma((14,)),
            dma((19,)), dma((32,)),
            dma((3,)), dma((3,)),
            dma((3,)), dma((3,)),
            dma((15,)), dma((15,)),
            dma((9,)),
        ],
        compiler_params=pltpu.CompilerParams(
            collective_id=0, has_side_effects=True, vmem_limit_bytes=60 * 1024 * 1024
        ),
        name="joint_attention",
    )(
        queries.T, key_rows.T, values.T, text_keys.T, text_values.T,
        block_image, gate_image, residual, w_out,
    )


def solution(mesh):
    placed = (
        P("blk", "head"),
        P("blk", "head"),
        P("blk", "head"),
        P(None, "head"),
        P(None, "head"),
        P(),
        P(),
        P(("blk", "head"), None),
        P("head", None),
    )
    return jax.shard_map(
        on_device, mesh=mesh, in_specs=placed, out_specs=P(("blk", "head"), None), check_vma=False
    )
```

time: 73.9 us -> 56.5 us (0.76)
  Pallas kernels: 72.2 us -> 54.8 us
    pallas_call x1, Pallas kernels: 72.2 us -> 54.8 us  [on_device(): pl.pallas_call(kernel, out_shape=jax.ShapeDtypeStruct((ROWS, D), BF), in_...]
where the time goes in v3:
time: 56.5 us; the launch traced here: 56.3 us
  Pallas kernels  54.8 us (97%)
  local copies, waits for them, and re-layouts  1.54 us (3%)
    pallas_call x1, Pallas kernels, on_device(): pl.pallas_call(kernel, out_shape=jax.ShapeDtypeStruct((ROWS, D), BF), in_...  54.8 us
    unnamed x1, local copies, waits for them, and re-layouts  1.54 us

profile of v3, /device:TPU:1, one launch (start us, length us, event | category | flops | bytes accessed | tf_op | source)
XLA Modules:
  0.0 56.3 jit_solution(1886398964813927973)
XLA Ops:
  0.0 54.8 %joint_attention.1 = bf16[32,1536]{1,0:T(8,128)(2,1)} custom-call(bf16[64,512]{1,0:T(8,128)(2,1)} %bitcast.7, bf16[64,512]{1,0:T(8,128)(2,1)} %bitcast.8, bf16[64,512]{1,0:T(8,128)(2,1)} %bitcast.9, bf16[64,1232]{1,0:T(8,128)(2,1)} %bitcast.5, bf16[64,1232]{1,0:T(8,128)(2,1)} %bitcast.6, s32[128]{0:T(128)} %img_hbm.1, f32[8,1536]{1,0:T(8,128)} %gate_hbm.1, ...), custom_call_target="tpu_custom_call" | custom-call | tf_op jit(solution)/shard_map/joint_attention/pallas_call | solution.py:361
  54.8 1.5 %copy.11 = bf16[32,1536]{1,0:T(8,128)(2,1)} copy(bf16[32,1536]{1,0:T(8,128)(2,1)} %joint_attention.1) | data formatting | bytes 196608

commit v4 on v3

--- a/solution.py
+++ b/solution.py
@@ -41,7 +41,7 @@
 def kernel(
     q_hbm, k_hbm, v_hbm, tk_hbm, tv_hbm, img_hbm, gate_hbm, res_hbm, w_hbm,
     out_ref,
-    img_ref, kv, qt, tk_ref, tv_ref, gate_ref, res_ref, qa, ka, va, acc, mx, tpad, s0, s1, osend, orecv, ssend, srecv, attl, atth, arecv, wbuf,
+    img_ref, kv, qt, tk_ref, tv_ref, gate_ref, res_ref, qa, ka, va, acc, mx, tpad, s0, s1, osend, orecv, ssend, srecv, packed, arecv, wbuf,
     q_s, q_r, kv_s, kv_r, w_s, w_r, o_s, o_r, st_s, st_r, a_s, a_r, in_s,
 ):
     blk = lax.axis_index("blk")
@@ -100,11 +100,11 @@
         dev = {"blk": zleft if kind in ("lk", "lv") else zright}
         kv_cps[kind, step] = send(kv.at[src, rows], kv.at[dst, rows], kv_s.at[k], kv_r.at[k], dev)
 
-    def kv_hop(step):
-        for kind, last in (("rk", 4), ("lk", 3), ("rv", 3), ("lv", 4)):
+    def kv_hop(part, step):
+        for kind in ("r" + part, "l" + part):
             if (kind, step) in kv_cps:
                 kv_cps[kind, step].wait_recv()
-                if step < last:
+                if (kind, step + 1) not in kv_cps and step < {"rk": 4, "lk": 3, "rv": 3, "lv": 4}[kind]:
                     kv_send(kind, step + 1)
 
     w_count = [0]
@@ -207,9 +207,6 @@
     tail = -(-(ntext - edge) // 128) * 128
     for cp in loads[:4]:
         cp.wait()
-    fill_queries(0)
-    fill_keys(0, blk * (TOK // BS))
-
     with jax.named_scope("barrier"):
         pl.semaphore_wait(barrier, 5 + NH - 1)
 
@@ -221,6 +218,8 @@
         w_copy(0, s)
     w_copy(0, 1)
 
+    fill_queries(0)
+    fill_keys(0, blk * (TOK // BS))
     loads[5].wait()
     loads[6].wait()
     for n, ref in ((0, tk_ref), (1, tv_ref)):
@@ -245,54 +244,60 @@
     fill_queries(1)
     steps((0, 1))
     flush()
-    with jax.named_scope("kvwait1"):
-        kv_hop(1)
+    with jax.named_scope("k1"):
+        kv_hop("k", 1)
+    with jax.named_scope("v1"):
+        kv_hop("v", 1)
     w_copy(0, 2, 0)
     fill_keys(7, origin_block(7))
     fill_keys(1, origin_block(1))
-    steps((7, 0), (1, 0), (7, 1), (1, 1))
-    flush()
+    steps((7, 1), (1, 1), (7, 0))
+    with jax.named_scope("k2"):
+        kv_hop("k", 2)
     with jax.named_scope("qwait2"):
         q_cps[2].wait_recv()
     w_copy(0, 2, 1)
     fill_queries(2)
     steps((0, 2), (7, 2), (1, 2))
-    flush()
-    with jax.named_scope("kvwait2"):
-        kv_hop(2)
+    with jax.named_scope("v2"):
+        kv_hop("v", 2)
     fill_keys(6, origin_block(6))
     fill_keys(2, origin_block(2))
-    steps((6, 0), (2, 0), (6, 1), (2, 1), (6, 2), (2, 2))
-    flush()
+    steps((6, 1), (2, 1), (6, 2), (2, 2))
+    with jax.named_scope("k3"):
+        kv_hop("k", 3)
     with jax.named_scope("qwait3"):
         q_cps[3].wait_recv()
     fill_queries(3)
     steps((0, 3), (7, 3), (1, 3))
-    flush()
-    with jax.named_scope("kvwait3"):
-        kv_hop(3)
+    with jax.named_scope("v3"):
+        kv_hop("v", 3)
     fill_keys(5, origin_block(5))
     fill_keys(3, origin_block(3))
-    steps((6, 3), (2, 3), (5, 0), (3, 0))
-    flush()
+    steps((6, 3), (2, 3), (5, 3), (3, 3))
+    with jax.named_scope("k4"):
+        kv_hop("k", 4)
+    steps((5, 2), (3, 2))
+    with jax.named_scope("v4"):
+        kv_hop("v", 4)
+    fill_keys(4, origin_block(4))
+    steps((4, 3), (4, 2))
+    send_part(3)
+    steps((5, 1))
+    send_part(2)
+    steps((3, 1), (4, 1))
     with jax.named_scope("wywait"):
         w_wait(2, 0)
     for s in (4, 12, 8):
         w_copy(2, s, 0)
+    steps((1, 0))
+    send_part(1)
+    steps((6, 0), (2, 0))
     for s in (4, 12, 8):
         w_wait(s)
         w_copy(s, 1)
-    with jax.named_scope("kvwait4"):
-        kv_hop(4)
-    fill_keys(4, origin_block(4))
-    with jax.named_scope("last"):
-        steps((5, 3), (3, 3), (4, 3), (5, 2))
-        send_part(3)
-        steps((3, 2), (4, 2), (5, 1))
-        send_part(2)
-        steps((3, 1), (4, 1), (4, 0))
-        send_part(1)
-        flush()
+    steps((5, 0), (3, 0), (4, 0))
+    flush()
     with jax.named_scope("wywait2"):
         w_wait(2, 1)
     for s in (4, 12, 8):
@@ -316,23 +321,24 @@
         numer = numer + orecv[c - 1].astype(F32) * scales[c]
     att = numer / denom
     both = jnp.concatenate([att, att], axis=0).T
-    side = iota((TOK, 128), 1) < HD
-    attl[...] = jnp.where(side, both, 0.0).astype(BF)
-    atth[...] = jnp.where(side, 0.0, both).astype(BF)
+    half = ROWS // 2
+    side = iota((half, 128), 1) < HD
+    for j in range(NH):
+        one = both[j * ROWS : j * ROWS + half]
+        two = both[j * ROWS + half : (j + 1) * ROWS]
+        packed[j] = jnp.where(side, one, two).astype(BF)
 
     a_cps = []
-    for s in range(1, NH):
-        src = atth if s % 2 else attl
-        start = pl.multiple_of(hpeer[s] * ROWS, ROWS)
+    for s in (10, 11, 2, 3, 6, 7, 14, 15, 8, 9, 4, 5, 12, 13, 1):
         a_cps.append(
-            send(src.at[pl.ds(start, ROWS)], arecv.at[s - 1], a_s.at[s - 1], a_r.at[s - 1], {"head": hpeer[s]})
+            send(packed.at[hpeer[s]], arecv.at[s - 1], a_s.at[s - 1], a_r.at[s - 1], {"head": hpeer[s]})
         )
     for s in (6, 14, 10):
         with jax.named_scope("wxwait2"):
             w_wait(s, 0)
             w_wait(s, 1)
         w_copy(s, 1)
-    mine = attl[pl.ds(pl.multiple_of(head * ROWS, ROWS), ROWS)]
+    mine = packed[head].astype(F32)
     with jax.named_scope("await"):
         for cp in a_cps:
             cp.wait_recv()
@@ -341,9 +347,13 @@
     with jax.named_scope("wcwait"):
         for s in (1, 5, 13, 9, 3, 7, 15, 11):
             w_wait(s)
-    pairs = [mine + arecv[0]]
-    for i in range(1, NH // 2):
-        pairs.append(arecv[2 * i - 1] + arecv[2 * i])
+    pairs = []
+    for i in range(NH // 2):
+        even = mine if i == 0 else arecv[2 * i - 1].astype(F32)
+        odd = arecv[2 * i].astype(F32)
+        upper = jnp.where(side, even, pltpu.roll(odd, HD, 1))
+        lower = jnp.where(side, pltpu.roll(even, HD, 1), odd)
+        pairs.append(jnp.concatenate([upper, lower], axis=0).astype(BF))
     mixed = jnp.concatenate(pairs, axis=1)
     image = img_ref[blk * (TOK // BS) + head // (NH * BS // TOK)]
     gating = gate_ref[pl.ds(image, 1), :]
@@ -383,9 +393,8 @@
             pltpu.VMEM((3, HD, TOK), BF),
             pltpu.VMEM((3, 8, 128), F32),
             pltpu.VMEM((3, 8, 128), F32),
-            pltpu.VMEM((TOK, 128), BF),
-            pltpu.VMEM((TOK, 128), BF),
-            pltpu.VMEM((NH - 1, ROWS, 128), BF),
+            pltpu.VMEM((NH, ROWS // 2, 128), BF),
+            pltpu.VMEM((NH - 1, ROWS // 2, 128), BF),
             pltpu.VMEM((NH * HD, D), BF),
             dma((3,)), dma((3,)),
             dma((14,)), dma((14,)),

time: 56.5 us -> 53.9 us (0.954)
  Pallas kernels: 54.8 us -> 52.2 us
    pallas_call x1, Pallas kernels: 54.8 us -> 52.2 us  [on_device(): pl.pallas_call(kernel, out_shape=jax.ShapeDtypeStruct((ROWS, D), BF), in_...]
where the time goes in v4:
time: 53.9 us; the launch traced here: 53.7 us
  Pallas kernels  52.2 us (97%)
  local copies, waits for them, and re-layouts  1.54 us (3%)
    pallas_call x1, Pallas kernels, on_device(): pl.pallas_call(kernel, out_shape=jax.ShapeDtypeStruct((ROWS, D), BF), in_...  52.2 us
    unnamed x1, local copies, waits for them, and re-layouts  1.54 us

profile of v4, /device:TPU:1, one launch (start us, length us, event | category | flops | bytes accessed | tf_op | source)
XLA Modules:
  0.0 53.7 jit_solution(13315825815087353089)
XLA Ops:
  0.0 52.2 %joint_attention.1 = bf16[32,1536]{1,0:T(8,128)(2,1)} custom-call(bf16[64,512]{1,0:T(8,128)(2,1)} %bitcast.7, bf16[64,512]{1,0:T(8,128)(2,1)} %bitcast.8, bf16[64,512]{1,0:T(8,128)(2,1)} %bitcast.9, bf16[64,1232]{1,0:T(8,128)(2,1)} %bitcast.5, bf16[64,1232]{1,0:T(8,128)(2,1)} %bitcast.6, s32[128]{0:T(128)} %img_hbm.1, f32[8,1536]{1,0:T(8,128)} %gate_hbm.1, ...), custom_call_target="tpu_custom_call" | custom-call | tf_op jit(solution)/shard_map/joint_attention/pallas_call | solution.py:371
  52.2 1.5 %copy.11 = bf16[32,1536]{1,0:T(8,128)(2,1)} copy(bf16[32,1536]{1,0:T(8,128)(2,1)} %joint_attention.1) | data formatting | bytes 196608

commit v5 on v4

--- a/solution.py
+++ b/solution.py
@@ -42,7 +42,7 @@
     q_hbm, k_hbm, v_hbm, tk_hbm, tv_hbm, img_hbm, gate_hbm, res_hbm, w_hbm,
     out_ref,
     img_ref, kv, qt, tk_ref, tv_ref, gate_ref, res_ref, qa, ka, va, acc, mx, tpad, s0, s1, osend, orecv, ssend, srecv, packed, arecv, wbuf,
-    q_s, q_r, kv_s, kv_r, w_s, w_r, o_s, o_r, st_s, st_r, a_s, a_r, in_s,
+    q_s, q_r, kv_s, kv_r, w_s, w_r, o_s, o_r, st_s, st_r, a_s, a_r, in_s, token,
 ):
     blk = lax.axis_index("blk")
     head = lax.axis_index("head")
@@ -56,7 +56,7 @@
     barrier = pltpu.get_barrier_semaphore()
     for other in (zright, zleft, ypeer[1], ypeer[2], ypeer[3]):
         pl.semaphore_signal(barrier, inc=1, device_id={"blk": other}, device_id_type=MESH)
-    for s in range(1, NH):
+    for s in (4, 12, 8, 2, 1):
         pl.semaphore_signal(barrier, inc=1, device_id={"head": hpeer[s]}, device_id_type=MESH)
 
     loads = [
@@ -92,20 +92,21 @@
 
     kv_cps = {}
 
-    def kv_send(kind, step):
+    def kv_send(kind, step, half):
         src = step - 1 if kind in ("lk", "lv") or step == 1 else ZL - (step - 1)
         dst = step if kind in ("lk", "lv") else ZL - step
-        k = {"rk": 0, "rv": 4, "lk": 7, "lv": 10}[kind] + step - 1
-        rows = pl.ds(0 if kind in ("rk", "lk") else HD, HD)
+        k = 2 * ({"rk": 0, "rv": 4, "lk": 7, "lv": 10}[kind] + step - 1) + half
+        rows = pl.ds((0 if kind in ("rk", "lk") else HD) + half * (HD // 2), HD // 2)
         dev = {"blk": zleft if kind in ("lk", "lv") else zright}
-        kv_cps[kind, step] = send(kv.at[src, rows], kv.at[dst, rows], kv_s.at[k], kv_r.at[k], dev)
+        kv_cps[kind, step, half] = send(kv.at[src, rows], kv.at[dst, rows], kv_s.at[k], kv_r.at[k], dev)
 
     def kv_hop(part, step):
-        for kind in ("r" + part, "l" + part):
-            if (kind, step) in kv_cps:
-                kv_cps[kind, step].wait_recv()
-                if (kind, step + 1) not in kv_cps and step < {"rk": 4, "lk": 3, "rv": 3, "lv": 4}[kind]:
-                    kv_send(kind, step + 1)
+        for half in range(2):
+            for kind in ("r" + part, "l" + part):
+                if (kind, step, half) in kv_cps:
+                    kv_cps[kind, step, half].wait_recv()
+                    if step < {"rk": 4, "lk": 3, "rv": 3, "lv": 4}[kind]:
+                        kv_send(kind, step + 1, half)
 
     w_count = [0]
 
@@ -208,11 +209,14 @@
     for cp in loads[:4]:
         cp.wait()
     with jax.named_scope("barrier"):
-        pl.semaphore_wait(barrier, 5 + NH - 1)
+        pl.semaphore_wait(barrier, 10)
 
     q_cps = [None] + [q_copy(c) for c in (1, 2, 3)]
-    for kind in ("rk", "lk", "rv", "lv"):
-        kv_send(kind, 1)
+    for part in ("k", "v"):
+        for half in range(2):
+            kv_send("r" + part, 1, half)
+            kv_send("l" + part, 1, half)
+    pl.semaphore_signal(token.at[0], inc=1, device_id={"head": hpeer[2]}, device_id_type=MESH)
     loads[4].wait()
     for s in (4, 12, 8):
         w_copy(0, s)
@@ -239,6 +243,7 @@
     with jax.named_scope("text"):
         steps((8, 0), (9, 0), (10, 0), (0, 0))
         flush()
+    w_copy(0, 2, 0)
     with jax.named_scope("qwait1"):
         q_cps[1].wait_recv()
     fill_queries(1)
@@ -248,15 +253,16 @@
         kv_hop("k", 1)
     with jax.named_scope("v1"):
         kv_hop("v", 1)
-    w_copy(0, 2, 0)
+    w_copy(0, 2, 1)
+    pl.semaphore_wait(token.at[0], 1)
+    pl.semaphore_signal(token.at[1], inc=1, device_id={"head": hpeer[1]}, device_id_type=MESH)
     fill_keys(7, origin_block(7))
     fill_keys(1, origin_block(1))
-    steps((7, 1), (1, 1), (7, 0))
+    steps((7, 1), (1, 1), (7, 0), (1, 0))
     with jax.named_scope("k2"):
         kv_hop("k", 2)
     with jax.named_scope("qwait2"):
         q_cps[2].wait_recv()
-    w_copy(0, 2, 1)
     fill_queries(2)
     steps((0, 2), (7, 2), (1, 2))
     with jax.named_scope("v2"):
@@ -275,34 +281,33 @@
     fill_keys(5, origin_block(5))
     fill_keys(3, origin_block(3))
     steps((6, 3), (2, 3), (5, 3), (3, 3))
+    with jax.named_scope("wywait"):
+        w_wait(2, 0)
+    for s in (4, 12, 8):
+        w_copy(2, s, 0)
     with jax.named_scope("k4"):
         kv_hop("k", 4)
-    steps((5, 2), (3, 2))
+    steps((5, 2), (3, 2), (5, 1))
     with jax.named_scope("v4"):
         kv_hop("v", 4)
     fill_keys(4, origin_block(4))
     steps((4, 3), (4, 2))
     send_part(3)
-    steps((5, 1))
+    steps((3, 1))
     send_part(2)
-    steps((3, 1), (4, 1))
-    with jax.named_scope("wywait"):
-        w_wait(2, 0)
-    for s in (4, 12, 8):
-        w_copy(2, s, 0)
-    steps((1, 0))
-    send_part(1)
-    steps((6, 0), (2, 0))
-    for s in (4, 12, 8):
-        w_wait(s)
-        w_copy(s, 1)
-    steps((5, 0), (3, 0), (4, 0))
-    flush()
     with jax.named_scope("wywait2"):
         w_wait(2, 1)
     for s in (4, 12, 8):
         w_copy(2, s, 1)
     w_copy(2, 1)
+    steps((4, 1), (6, 0))
+    send_part(1)
+    for s in (4, 12, 8):
+        w_wait(s)
+        w_copy(s, 1)
+    steps((2, 0), (5, 0), (3, 0), (4, 0))
+    flush()
+    pl.semaphore_wait(token.at[1], 1)
     with jax.named_scope("owait"):
         for c in (1, 2, 3):
             o_cps[c].wait_recv()
@@ -397,12 +402,13 @@
             pltpu.VMEM((NH - 1, ROWS // 2, 128), BF),
             pltpu.VMEM((NH * HD, D), BF),
             dma((3,)), dma((3,)),
-            dma((14,)), dma((14,)),
+            dma((28,)), dma((28,)),
             dma((19,)), dma((32,)),
             dma((3,)), dma((3,)),
             dma((3,)), dma((3,)),
             dma((15,)), dma((15,)),
             dma((9,)),
+            pltpu.SemaphoreType.REGULAR((2,)),
         ],
         compiler_params=pltpu.CompilerParams(
             collective_id=0, has_side_effects=True, vmem_limit_bytes=60 * 1024 * 1024

time: 53.9 us -> 52.2 us (0.968)
  Pallas kernels: 52.2 us -> 50.5 us
    pallas_call x1, Pallas kernels: 52.2 us -> 50.5 us  [on_device(): pl.pallas_call(kernel, out_shape=jax.ShapeDtypeStruct((ROWS, D), BF), in_...]
where the time goes in v5:
time: 52.2 us; the launch traced here: 52 us
  Pallas kernels  50.5 us (97%)
  local copies, waits for them, and re-layouts  1.54 us (3%)
    pallas_call x1, Pallas kernels, on_device(): pl.pallas_call(kernel, out_shape=jax.ShapeDtypeStruct((ROWS, D), BF), in_...  50.5 us
    unnamed x1, local copies, waits for them, and re-layouts  1.54 us

profile of v5, /device:TPU:1, one launch (start us, length us, event | category | flops | bytes accessed | tf_op | source)
XLA Modules:
  0.0 52.0 jit_solution(13111913854027717804)
XLA Ops:
  0.0 50.5 %joint_attention.1 = bf16[32,1536]{1,0:T(8,128)(2,1)} custom-call(bf16[64,512]{1,0:T(8,128)(2,1)} %bitcast.7, bf16[64,512]{1,0:T(8,128)(2,1)} %bitcast.8, bf16[64,512]{1,0:T(8,128)(2,1)} %bitcast.9, bf16[64,1232]{1,0:T(8,128)(2,1)} %bitcast.5, bf16[64,1232]{1,0:T(8,128)(2,1)} %bitcast.6, s32[128]{0:T(128)} %img_hbm.1, f32[8,1536]{1,0:T(8,128)} %gate_hbm.1, ...), custom_call_target="tpu_custom_call" | custom-call | tf_op jit(solution)/shard_map/joint_attention/pallas_call | solution.py:376
  50.5 1.5 %copy.11 = bf16[32,1536]{1,0:T(8,128)(2,1)} copy(bf16[32,1536]{1,0:T(8,128)(2,1)} %joint_attention.1) | data formatting | bytes 196608

commit v6 on v5

--- a/solution.py
+++ b/solution.py
@@ -243,26 +243,25 @@
     with jax.named_scope("text"):
         steps((8, 0), (9, 0), (10, 0), (0, 0))
         flush()
-    w_copy(0, 2, 0)
-    with jax.named_scope("qwait1"):
-        q_cps[1].wait_recv()
-    fill_queries(1)
-    steps((0, 1))
-    flush()
     with jax.named_scope("k1"):
         kv_hop("k", 1)
     with jax.named_scope("v1"):
         kv_hop("v", 1)
-    w_copy(0, 2, 1)
+    fill_keys(7, origin_block(7))
+    fill_keys(1, origin_block(1))
+    steps((7, 0), (1, 0))
+    with jax.named_scope("qwait1"):
+        q_cps[1].wait_recv()
+    w_copy(0, 2, 0)
     pl.semaphore_wait(token.at[0], 1)
     pl.semaphore_signal(token.at[1], inc=1, device_id={"head": hpeer[1]}, device_id_type=MESH)
-    fill_keys(7, origin_block(7))
-    fill_keys(1, origin_block(1))
-    steps((7, 1), (1, 1), (7, 0), (1, 0))
+    fill_queries(1)
+    steps((0, 1), (7, 1), (1, 1))
     with jax.named_scope("k2"):
         kv_hop("k", 2)
     with jax.named_scope("qwait2"):
         q_cps[2].wait_recv()
+    w_copy(0, 2, 1)
     fill_queries(2)
     steps((0, 2), (7, 2), (1, 2))
     with jax.named_scope("v2"):
@@ -272,40 +271,42 @@
     steps((6, 1), (2, 1), (6, 2), (2, 2))
     with jax.named_scope("k3"):
         kv_hop("k", 3)
-    with jax.named_scope("qwait3"):
-        q_cps[3].wait_recv()
-    fill_queries(3)
-    steps((0, 3), (7, 3), (1, 3))
+    steps((6, 0), (2, 0))
     with jax.named_scope("v3"):
         kv_hop("v", 3)
     fill_keys(5, origin_block(5))
     fill_keys(3, origin_block(3))
-    steps((6, 3), (2, 3), (5, 3), (3, 3))
+    steps((5, 1), (3, 1))
+    with jax.named_scope("qwait3"):
+        q_cps[3].wait_recv()
+    fill_queries(3)
+    steps((0, 3), (7, 3))
+    with jax.named_scope("k4"):
+        kv_hop("k", 4)
+    for s in (4, 12, 8):
+        w_wait(s)
+        w_copy(s, 1)
+    steps((1, 3), (6, 3), (2, 3))
+    with jax.named_scope("v4"):
+        kv_hop("v", 4)
+    fill_keys(4, origin_block(4))
+    steps((5, 3), (3, 3))
     with jax.named_scope("wywait"):
         w_wait(2, 0)
     for s in (4, 12, 8):
         w_copy(2, s, 0)
-    with jax.named_scope("k4"):
-        kv_hop("k", 4)
-    steps((5, 2), (3, 2), (5, 1))
-    with jax.named_scope("v4"):
-        kv_hop("v", 4)
-    fill_keys(4, origin_block(4))
-    steps((4, 3), (4, 2))
+    steps((4, 3), (5, 2))
     send_part(3)
-    steps((3, 1))
+    steps((3, 2), (4, 2), (4, 1))
     send_part(2)
     with jax.named_scope("wywait2"):
         w_wait(2, 1)
     for s in (4, 12, 8):
         w_copy(2, s, 1)
     w_copy(2, 1)
-    steps((4, 1), (6, 0))
+    steps((5, 0))
     send_part(1)
-    for s in (4, 12, 8):
-        w_wait(s)
-        w_copy(s, 1)
-    steps((2, 0), (5, 0), (3, 0), (4, 0))
+    steps((3, 0), (4, 0))
     flush()
     pl.semaphore_wait(token.at[1], 1)
     with jax.named_scope("owait"):
@@ -375,7 +376,7 @@
     dma = pltpu.SemaphoreType.DMA
     return pl.pallas_call(
         kernel,
-        out_shape=jax.ShapeDtypeStruct((ROWS, D), BF),
+        out_shape=pltpu.VMEM((ROWS, D), BF),
         in_specs=[hb] * 9,
         out_specs=vm,
         scratch_shapes=[

time: 52.2 us -> 48.3 us (0.925)
  Pallas kernels: 50.5 us -> 47.5 us
  local copies, waits for them, and re-layouts: 1.54 us -> 0.64 us
    pallas_call x1, Pallas kernels: 50.5 us -> 47.5 us  [on_device(): pl.pallas_call(kernel, out_shape=pltpu.VMEM((ROWS, D), BF), in_specs=[hb]...]
    unnamed x1, local copies, waits for them, and re-layouts: 1.54 us -> 0.64 us
where the time goes in v6:
time: 48.3 us; the launch traced here: 48.1 us
  Pallas kernels  47.5 us (98%)
  local copies, waits for them, and re-layouts  0.64 us (1%)
    pallas_call x1, Pallas kernels, on_device(): pl.pallas_call(kernel, out_shape=pltpu.VMEM((ROWS, D), BF), in_specs=[hb]...  47.5 us

profile of v6, /device:TPU:1, one launch (start us, length us, event | category | flops | bytes accessed | tf_op | source)
XLA Modules:
  0.0 48.1 jit_solution(427917996822284537)
XLA Ops:
  0.0 47.5 %joint_attention.1 = bf16[32,1536]{1,0:T(8,128)(2,1)S(1)} custom-call(bf16[64,512]{1,0:T(8,128)(2,1)} %bitcast.7, bf16[64,512]{1,0:T(8,128)(2,1)} %bitcast.8, bf16[64,512]{1,0:T(8,128)(2,1)} %bitcast.9, bf16[64,1232]{1,0:T(8,128)(2,1)} %bitcast.5, bf16[64,1232]{1,0:T(8,128)(2,1)} %bitcast.6, s32[128]{0:T(128)} %img_hbm.1, f32[8,1536]{1,0:T(8,128)} %gate_hbm.1, ...), custom_call_target="tpu_custom_call" | custom-call | tf_op jit(solution)/shard_map/joint_attention/pallas_call | solution.py:377
  47.5 0.6 %copy.11 = bf16[32,1536]{1,0:T(8,128)(2,1)} copy(bf16[32,1536]{1,0:T(8,128)(2,1)S(1)} %joint_attention.1) | data formatting | bytes 196608

commit v7 on v6

--- a/solution.py
+++ b/solution.py
@@ -29,7 +29,7 @@
 def flip(index, mask, bits):
     total = 0
     for b in range(bits):
-        bit = (index // (1 << b)) % 2
+        bit = lax.rem(lax.div(index, 1 << b), 2)
         total = total + (1 << b) * ((1 - bit) if (mask >> b) & 1 else bit)
     return total
 
@@ -46,10 +46,10 @@
 ):
     blk = lax.axis_index("blk")
     head = lax.axis_index("head")
-    z = blk // YL
-    y = blk % YL
-    zright = ((z + 1) % ZL) * YL + y
-    zleft = ((z + ZL - 1) % ZL) * YL + y
+    z = lax.div(blk, YL)
+    y = lax.rem(blk, YL)
+    zright = lax.rem(z + 1, ZL) * YL + y
+    zleft = lax.rem(z + ZL - 1, ZL) * YL + y
     ypeer = [z * YL + flip(y, c, 2) for c in range(YL)]
     hpeer = [flip(head, s, 4) for s in range(NH)]
 
@@ -76,19 +76,26 @@
     for cp in loads:
         cp.start()
 
-    started = []
-
     def send(src, dst, ssem, rsem, dev):
         copy = pltpu.make_async_remote_copy(
             src_ref=src, dst_ref=dst, send_sem=ssem, recv_sem=rsem,
             device_id=dev, device_id_type=MESH,
         )
         copy.start()
-        started.append(copy)
         return copy
 
+    def settle(ref, sem, sent=False):
+        copy = pltpu.make_async_remote_copy(
+            src_ref=ref, dst_ref=ref, send_sem=sem, recv_sem=sem,
+            device_id={"head": hpeer[1]}, device_id_type=MESH,
+        )
+        if sent:
+            copy.wait_send()
+        else:
+            copy.wait_recv()
+
     def q_copy(c):
-        return send(qt.at[0], qt.at[c], q_s.at[c - 1], q_r.at[c - 1], {"blk": ypeer[c]})
+        return send(qt.at[0], qt.at[c], q_s, q_r.at[c - 1], {"blk": ypeer[c]})
 
     kv_cps = {}
 
@@ -98,7 +105,7 @@
         k = 2 * ({"rk": 0, "rv": 4, "lk": 7, "lv": 10}[kind] + step - 1) + half
         rows = pl.ds((0 if kind in ("rk", "lk") else HD) + half * (HD // 2), HD // 2)
         dev = {"blk": zleft if kind in ("lk", "lv") else zright}
-        kv_cps[kind, step, half] = send(kv.at[src, rows], kv.at[dst, rows], kv_s.at[k], kv_r.at[k], dev)
+        kv_cps[kind, step, half] = send(kv.at[src, rows], kv.at[dst, rows], kv_s, kv_r.at[k], dev)
 
     def kv_hop(part, step):
         for half in range(2):
@@ -108,28 +115,20 @@
                     if step < {"rk": 4, "lk": 3, "rv": 3, "lv": 4}[kind]:
                         kv_send(kind, step + 1, half)
 
-    w_count = [0]
-
     def w_part(slot, half):
         if half is None:
             return wbuf.at[pl.ds(slot * HD, HD)]
         return wbuf.at[pl.ds(slot * HD + half * (HD // 2), HD // 2)]
 
-    def w_sem(slot, half):
-        return w_r.at[slot if half in (None, 0) else NH + slot]
-
     def w_copy(origin, to, half=None):
         slot = origin ^ to
-        k = w_count[0]
-        w_count[0] += 1
-        return send(w_part(origin, half), w_part(slot, half), w_s.at[k], w_sem(slot, half), {"head": hpeer[to]})
-
-    def w_wait(slot, half=None):
-        part = w_part(slot, half)
-        pltpu.make_async_remote_copy(
-            src_ref=part, dst_ref=part, send_sem=w_s.at[0], recv_sem=w_sem(slot, half),
-            device_id={"head": hpeer[1]}, device_id_type=MESH,
-        ).wait_recv()
+        if slot == 2:
+            sem = w_r.at[half]
+        elif slot % 2:
+            sem = w_r.at[2]
+        else:
+            sem = w_r.at[3 if slot in (4, 12, 8) else 4]
+        send(w_part(origin, half), w_part(slot, half), w_s, sem, {"head": hpeer[to]})
 
     def fill_keys(slot, first_block):
         row = iota((HD, BS), 0)
@@ -189,10 +188,7 @@
             pending.append((slot, c, n, buf))
 
     def origin_block(slot):
-        return (((z + slot) % ZL) * YL + y) * (TOK // BS)
-
-    o_cps = [None] * YL
-    st_cps = [None] * YL
+        return (lax.rem(z + slot, ZL) * YL + y) * (TOK // BS)
 
     def send_part(c):
         osend[c - 1] = acc[c, 0:HD].astype(BF)
@@ -200,8 +196,8 @@
             ssend[c - 1, a : a + 1] = mx[c, 0:1, a * 128 : (a + 1) * 128]
             ssend[c - 1, 4 + a : 5 + a] = acc[c, HD : HD + 1, a * 128 : (a + 1) * 128]
         dev = {"blk": ypeer[c]}
-        o_cps[c] = send(osend.at[c - 1], orecv.at[c - 1], o_s.at[c - 1], o_r.at[c - 1], dev)
-        st_cps[c] = send(ssend.at[c - 1], srecv.at[c - 1], st_s.at[c - 1], st_r.at[c - 1], dev)
+        send(osend.at[c - 1], orecv.at[c - 1], o_s, o_r, dev)
+        send(ssend.at[c - 1], srecv.at[c - 1], st_s, st_r, dev)
 
     ntext = tk_hbm.shape[1]
     edge = (TSLOTS - 1) * TOK
@@ -283,8 +279,8 @@
     steps((0, 3), (7, 3))
     with jax.named_scope("k4"):
         kv_hop("k", 4)
+    settle(wbuf.at[pl.ds(0, 3 * HD)], w_r.at[3])
     for s in (4, 12, 8):
-        w_wait(s)
         w_copy(s, 1)
     steps((1, 3), (6, 3), (2, 3))
     with jax.named_scope("v4"):
@@ -292,7 +288,7 @@
     fill_keys(4, origin_block(4))
     steps((5, 3), (3, 3))
     with jax.named_scope("wywait"):
-        w_wait(2, 0)
+        settle(w_part(2, 0), w_r.at[0])
     for s in (4, 12, 8):
         w_copy(2, s, 0)
     steps((4, 3), (5, 2))
@@ -300,7 +296,7 @@
     steps((3, 2), (4, 2), (4, 1))
     send_part(2)
     with jax.named_scope("wywait2"):
-        w_wait(2, 1)
+        settle(w_part(2, 1), w_r.at[1])
     for s in (4, 12, 8):
         w_copy(2, s, 1)
     w_copy(2, 1)
@@ -310,9 +306,8 @@
     flush()
     pl.semaphore_wait(token.at[1], 1)
     with jax.named_scope("owait"):
-        for c in (1, 2, 3):
-            o_cps[c].wait_recv()
-            st_cps[c].wait_recv()
+        settle(orecv, o_r)
+        settle(srecv, st_r)
 
     def row_of(ref, c, first):
         return jnp.concatenate([ref[c - 1, first + a : first + a + 1] for a in range(4)], axis=1)
@@ -334,25 +329,19 @@
         two = both[j * ROWS + half : (j + 1) * ROWS]
         packed[j] = jnp.where(side, one, two).astype(BF)
 
-    a_cps = []
     for s in (10, 11, 2, 3, 6, 7, 14, 15, 8, 9, 4, 5, 12, 13, 1):
-        a_cps.append(
-            send(packed.at[hpeer[s]], arecv.at[s - 1], a_s.at[s - 1], a_r.at[s - 1], {"head": hpeer[s]})
-        )
+        send(packed.at[hpeer[s]], arecv.at[s - 1], a_s, a_r, {"head": hpeer[s]})
+    with jax.named_scope("wxwait2"):
+        settle(wbuf.at[pl.ds(0, 3 * HD)], w_r.at[4])
     for s in (6, 14, 10):
-        with jax.named_scope("wxwait2"):
-            w_wait(s, 0)
-            w_wait(s, 1)
         w_copy(s, 1)
     mine = packed[head].astype(F32)
     with jax.named_scope("await"):
-        for cp in a_cps:
-            cp.wait_recv()
+        settle(arecv, a_r)
     loads[7].wait()
     loads[8].wait()
     with jax.named_scope("wcwait"):
-        for s in (1, 5, 13, 9, 3, 7, 15, 11):
-            w_wait(s)
+        settle(wbuf.at[pl.ds(0, NH // 2 * HD)], w_r.at[2])
     pairs = []
     for i in range(NH // 2):
         even = mine if i == 0 else arecv[2 * i - 1].astype(F32)
@@ -361,13 +350,17 @@
         lower = jnp.where(side, pltpu.roll(even, HD, 1), odd)
         pairs.append(jnp.concatenate([upper, lower], axis=0).astype(BF))
     mixed = jnp.concatenate(pairs, axis=1)
-    image = img_ref[blk * (TOK // BS) + head // (NH * BS // TOK)]
+    image = img_ref[blk * (TOK // BS) + lax.div(head, NH * BS // TOK)]
     gating = gate_ref[pl.ds(image, 1), :]
     projected = jnp.dot(mixed, wbuf[...], preferred_element_type=F32)
     out_ref[...] = (res_ref[...].astype(F32) + gating * projected).astype(BF)
     with jax.named_scope("sendwait"):
-        for cp in started:
-            cp.wait_send()
+        settle(qt.at[pl.ds(1, 3)], q_s, True)
+        settle(kv.at[pl.ds(0, 7)], kv_s, True)
+        settle(wbuf.at[pl.ds(0, 15 * HD)], w_s, True)
+        settle(osend, o_s, True)
+        settle(ssend, st_s, True)
+        settle(arecv, a_s, True)
 
 
 def on_device(queries, key_rows, values, text_keys, text_values, block_image, gate_image, residual, w_out):
@@ -402,12 +395,12 @@
             pltpu.VMEM((NH, ROWS // 2, 128), BF),
             pltpu.VMEM((NH - 1, ROWS // 2, 128), BF),
             pltpu.VMEM((NH * HD, D), BF),
-            dma((3,)), dma((3,)),
-            dma((28,)), dma((28,)),
-            dma((19,)), dma((32,)),
-            dma((3,)), dma((3,)),
-            dma((3,)), dma((3,)),
-            dma((15,)), dma((15,)),
+            dma, dma((3,)),
+            dma, dma((28,)),
+            dma, dma((5,)),
+            dma, dma,
+            dma, dma,
+            dma, dma,
             dma((9,)),
             pltpu.SemaphoreType.REGULAR((2,)),
         ],

time: 48.3 us -> 47.1 us (0.975)
  Pallas kernels: 47.5 us -> 46.3 us
    pallas_call x1, Pallas kernels: 47.5 us -> 46.3 us  [on_device(): pl.pallas_call(kernel, out_shape=pltpu.VMEM((ROWS, D), BF), in_specs=[hb]...]
where the time goes in v7:
time: 47.1 us; the launch traced here: 47 us
  Pallas kernels  46.3 us (98%)
  local copies, waits for them, and re-layouts  0.64 us (1%)
    pallas_call x1, Pallas kernels, on_device(): pl.pallas_call(kernel, out_shape=pltpu.VMEM((ROWS, D), BF), in_specs=[hb]...  46.3 us

profile of v7, /device:TPU:1, one launch (start us, length us, event | category | flops | bytes accessed | tf_op | source)
XLA Modules:
  0.0 47.0 jit_solution(6509666766693379096)
XLA Ops:
  0.0 46.3 %joint_attention.1 = bf16[32,1536]{1,0:T(8,128)(2,1)S(1)} custom-call(bf16[64,512]{1,0:T(8,128)(2,1)} %bitcast.7, bf16[64,512]{1,0:T(8,128)(2,1)} %bitcast.8, bf16[64,512]{1,0:T(8,128)(2,1)} %bitcast.9, bf16[64,1232]{1,0:T(8,128)(2,1)} %bitcast.5, bf16[64,1232]{1,0:T(8,128)(2,1)} %bitcast.6, s32[128]{0:T(128)} %img_hbm.1, f32[8,1536]{1,0:T(8,128)} %gate_hbm.1, ...), custom_call_target="tpu_custom_call" | custom-call | tf_op jit(solution)/shard_map/joint_attention/pallas_call | solution.py:370
  46.3 0.6 %copy.11 = bf16[32,1536]{1,0:T(8,128)(2,1)} copy(bf16[32,1536]{1,0:T(8,128)(2,1)S(1)} %joint_attention.1) | data formatting | bytes 196608

commit v8 on v7

--- a/solution.py
+++ b/solution.py
@@ -18,6 +18,7 @@
 D = 1536
 ROWS = TOK // NH
 TSLOTS = 3
+WQ = 4
 FAR = -(2.0**100)
 RATE = math.log2(math.e) / math.sqrt(HD)
 MESH = pl.DeviceIdType.MESH
@@ -118,16 +119,16 @@
     def w_part(slot, half):
         if half is None:
             return wbuf.at[pl.ds(slot * HD, HD)]
-        return wbuf.at[pl.ds(slot * HD + half * (HD // 2), HD // 2)]
+        return wbuf.at[pl.ds(slot * HD + half * (HD // WQ), HD // WQ)]
 
     def w_copy(origin, to, half=None):
         slot = origin ^ to
         if slot == 2:
             sem = w_r.at[half]
         elif slot % 2:
-            sem = w_r.at[2]
+            sem = w_r.at[WQ]
         else:
-            sem = w_r.at[3 if slot in (4, 12, 8) else 4]
+            sem = w_r.at[WQ + 1 if slot in (4, 12, 8) else WQ + 2]
         send(w_part(origin, half), w_part(slot, half), w_s, sem, {"head": hpeer[to]})
 
     def fill_keys(slot, first_block):
@@ -262,47 +263,50 @@
     steps((0, 2), (7, 2), (1, 2))
     with jax.named_scope("v2"):
         kv_hop("v", 2)
+    w_copy(0, 2, 2)
     fill_keys(6, origin_block(6))
     fill_keys(2, origin_block(2))
     steps((6, 1), (2, 1), (6, 2), (2, 2))
     with jax.named_scope("k3"):
         kv_hop("k", 3)
-    steps((6, 0), (2, 0))
+    w_copy(0, 2, 3)
+    with jax.named_scope("qwait3"):
+        q_cps[3].wait_recv()
+    fill_queries(3)
+    steps((0, 3), (7, 3))
+    steps((1, 3))
     with jax.named_scope("v3"):
         kv_hop("v", 3)
     fill_keys(5, origin_block(5))
     fill_keys(3, origin_block(3))
-    steps((5, 1), (3, 1))
-    with jax.named_scope("qwait3"):
-        q_cps[3].wait_recv()
-    fill_queries(3)
-    steps((0, 3), (7, 3))
+    steps((5, 1), (3, 1), (6, 3), (2, 3))
+    def w_hop(quarter):
+        with jax.named_scope("wy%d" % quarter):
+            settle(w_part(2, quarter), w_r.at[quarter])
+        for s in (4, 12, 8):
+            w_copy(2, s, quarter)
+
     with jax.named_scope("k4"):
         kv_hop("k", 4)
-    settle(wbuf.at[pl.ds(0, 3 * HD)], w_r.at[3])
+    settle(wbuf.at[pl.ds(0, 3 * HD)], w_r.at[WQ + 1])
     for s in (4, 12, 8):
         w_copy(s, 1)
-    steps((1, 3), (6, 3), (2, 3))
+    w_hop(0)
+    steps((5, 3), (3, 3))
     with jax.named_scope("v4"):
         kv_hop("v", 4)
+    w_hop(1)
     fill_keys(4, origin_block(4))
-    steps((5, 3), (3, 3))
-    with jax.named_scope("wywait"):
-        settle(w_part(2, 0), w_r.at[0])
-    for s in (4, 12, 8):
-        w_copy(2, s, 0)
     steps((4, 3), (5, 2))
     send_part(3)
+    w_hop(2)
     steps((3, 2), (4, 2), (4, 1))
     send_part(2)
-    with jax.named_scope("wywait2"):
-        settle(w_part(2, 1), w_r.at[1])
-    for s in (4, 12, 8):
-        w_copy(2, s, 1)
+    w_hop(3)
     w_copy(2, 1)
     steps((5, 0))
     send_part(1)
-    steps((3, 0), (4, 0))
+    steps((3, 0), (4, 0), (6, 0), (2, 0))
     flush()
     pl.semaphore_wait(token.at[1], 1)
     with jax.named_scope("owait"):
@@ -332,7 +336,7 @@
     for s in (10, 11, 2, 3, 6, 7, 14, 15, 8, 9, 4, 5, 12, 13, 1):
         send(packed.at[hpeer[s]], arecv.at[s - 1], a_s, a_r, {"head": hpeer[s]})
     with jax.named_scope("wxwait2"):
-        settle(wbuf.at[pl.ds(0, 3 * HD)], w_r.at[4])
+        settle(wbuf.at[pl.ds(0, 3 * HD)], w_r.at[WQ + 2])
     for s in (6, 14, 10):
         w_copy(s, 1)
     mine = packed[head].astype(F32)
@@ -341,7 +345,7 @@
     loads[7].wait()
     loads[8].wait()
     with jax.named_scope("wcwait"):
-        settle(wbuf.at[pl.ds(0, NH // 2 * HD)], w_r.at[2])
+        settle(wbuf.at[pl.ds(0, NH // 2 * HD)], w_r.at[WQ])
     pairs = []
     for i in range(NH // 2):
         even = mine if i == 0 else arecv[2 * i - 1].astype(F32)
@@ -397,7 +401,7 @@
             pltpu.VMEM((NH * HD, D), BF),
             dma, dma((3,)),
             dma, dma((28,)),
-            dma, dma((5,)),
+            dma, dma((WQ + 3,)),
             dma, dma,
             dma, dma,
             dma, dma,

time: 47.1 us -> 46.2 us (0.981)
  Pallas kernels: 46.3 us -> 45.4 us
    pallas_call x1, Pallas kernels: 46.3 us -> 45.4 us  [on_device(): pl.pallas_call(kernel, out_shape=pltpu.VMEM((ROWS, D), BF), in_specs=[hb]...]
where the time goes in v8:
time: 46.2 us; the launch traced here: 46 us
  Pallas kernels  45.4 us (98%)
  local copies, waits for them, and re-layouts  0.64 us (1%)
    pallas_call x1, Pallas kernels, on_device(): pl.pallas_call(kernel, out_shape=pltpu.VMEM((ROWS, D), BF), in_specs=[hb]...  45.4 us

profile of v8, /device:TPU:1, one launch (start us, length us, event | category | flops | bytes accessed | tf_op | source)
XLA Modules:
  0.0 46.0 jit_solution(8056448743842000905)
XLA Ops:
  0.0 45.4 %joint_attention.1 = bf16[32,1536]{1,0:T(8,128)(2,1)S(1)} custom-call(bf16[64,512]{1,0:T(8,128)(2,1)} %bitcast.7, bf16[64,512]{1,0:T(8,128)(2,1)} %bitcast.8, bf16[64,512]{1,0:T(8,128)(2,1)} %bitcast.9, bf16[64,1232]{1,0:T(8,128)(2,1)} %bitcast.5, bf16[64,1232]{1,0:T(8,128)(2,1)} %bitcast.6, s32[128]{0:T(128)} %img_hbm.1, f32[8,1536]{1,0:T(8,128)} %gate_hbm.1, ...), custom_call_target="tpu_custom_call" | custom-call | tf_op jit(solution)/shard_map/joint_attention/pallas_call | solution.py:374
  45.4 0.6 %copy.11 = bf16[32,1536]{1,0:T(8,128)(2,1)} copy(bf16[32,1536]{1,0:T(8,128)(2,1)S(1)} %joint_attention.1) | data formatting | bytes 196608

commit v9 on v8

--- a/solution.py
+++ b/solution.py
@@ -139,6 +139,8 @@
             gaps.append(jnp.where((row < 8) & (row != image), FAR, 0.0))
         wide = jnp.concatenate([kv[slot, 0:HD].astype(F32), jnp.concatenate(gaps, axis=1)], axis=0)
         ka[slot] = wide.T.astype(BF)
+
+    def fill_values(slot):
         va[slot, 0:HD] = kv[slot, HD : 2 * HD]
         va[slot, HD : HD + 16] = jnp.ones((16, TOK), BF)
 
@@ -221,6 +223,7 @@
 
     fill_queries(0)
     fill_keys(0, blk * (TOK // BS))
+    fill_values(0)
     loads[5].wait()
     loads[6].wait()
     for n, ref in ((0, tk_ref), (1, tv_ref)):
@@ -240,13 +243,22 @@
     with jax.named_scope("text"):
         steps((8, 0), (9, 0), (10, 0), (0, 0))
         flush()
+    def w_hop(quarter):
+        with jax.named_scope("wy%d" % quarter):
+            settle(w_part(2, quarter), w_r.at[quarter])
+        for s in (4, 12, 8):
+            w_copy(2, s, quarter)
+
     with jax.named_scope("k1"):
         kv_hop("k", 1)
+    fill_keys(7, origin_block(7))
+    fill_keys(1, origin_block(1))
+    steps((7, 0))
     with jax.named_scope("v1"):
         kv_hop("v", 1)
-    fill_keys(7, origin_block(7))
-    fill_keys(1, origin_block(1))
-    steps((7, 0), (1, 0))
+    fill_values(7)
+    fill_values(1)
+    steps((1, 0))
     with jax.named_scope("qwait1"):
         q_cps[1].wait_recv()
     w_copy(0, 2, 0)
@@ -256,6 +268,8 @@
     steps((0, 1), (7, 1), (1, 1))
     with jax.named_scope("k2"):
         kv_hop("k", 2)
+    fill_keys(6, origin_block(6))
+    fill_keys(2, origin_block(2))
     with jax.named_scope("qwait2"):
         q_cps[2].wait_recv()
     w_copy(0, 2, 1)
@@ -264,48 +278,44 @@
     with jax.named_scope("v2"):
         kv_hop("v", 2)
     w_copy(0, 2, 2)
-    fill_keys(6, origin_block(6))
-    fill_keys(2, origin_block(2))
+    fill_values(6)
+    fill_values(2)
     steps((6, 1), (2, 1), (6, 2), (2, 2))
     with jax.named_scope("k3"):
         kv_hop("k", 3)
+    fill_keys(5, origin_block(5))
+    fill_keys(3, origin_block(3))
     w_copy(0, 2, 3)
     with jax.named_scope("qwait3"):
         q_cps[3].wait_recv()
     fill_queries(3)
-    steps((0, 3), (7, 3))
-    steps((1, 3))
+    steps((0, 3), (7, 3), (1, 3), (5, 1))
     with jax.named_scope("v3"):
         kv_hop("v", 3)
-    fill_keys(5, origin_block(5))
-    fill_keys(3, origin_block(3))
-    steps((5, 1), (3, 1), (6, 3), (2, 3))
-    def w_hop(quarter):
-        with jax.named_scope("wy%d" % quarter):
-            settle(w_part(2, quarter), w_r.at[quarter])
-        for s in (4, 12, 8):
-            w_copy(2, s, quarter)
-
+    fill_values(5)
+    fill_values(3)
+    steps((3, 1), (6, 3), (2, 3))
     with jax.named_scope("k4"):
         kv_hop("k", 4)
+    fill_keys(4, origin_block(4))
     settle(wbuf.at[pl.ds(0, 3 * HD)], w_r.at[WQ + 1])
     for s in (4, 12, 8):
         w_copy(s, 1)
     w_hop(0)
-    steps((5, 3), (3, 3))
+    steps((5, 3), (3, 3), (5, 2), (3, 2), (4, 3))
     with jax.named_scope("v4"):
         kv_hop("v", 4)
     w_hop(1)
-    fill_keys(4, origin_block(4))
-    steps((4, 3), (5, 2))
+    fill_values(4)
+    steps((4, 2))
     send_part(3)
     w_hop(2)
-    steps((3, 2), (4, 2), (4, 1))
+    steps((4, 1))
     send_part(2)
+    steps((5, 0))
+    send_part(1)
     w_hop(3)
     w_copy(2, 1)
-    steps((5, 0))
-    send_part(1)
     steps((3, 0), (4, 0), (6, 0), (2, 0))
     flush()
     pl.semaphore_wait(token.at[1], 1)

time: 46.2 us -> 46.2 us (level)
  no operation moved by 1% of the time
where the time goes in v9:
time: 46.2 us; the launch traced here: 46 us
  Pallas kernels  45.4 us (98%)
  local copies, waits for them, and re-layouts  0.64 us (1%)
    pallas_call x1, Pallas kernels, on_device(): pl.pallas_call(kernel, out_shape=pltpu.VMEM((ROWS, D), BF), in_specs=[hb]...  45.4 us

profile of v9, /device:TPU:1, one launch (start us, length us, event | category | flops | bytes accessed | tf_op | source)
XLA Modules:
  0.0 46.0 jit_solution(18231742236580298314)
XLA Ops:
  0.0 45.4 %joint_attention.1 = bf16[32,1536]{1,0:T(8,128)(2,1)S(1)} custom-call(bf16[64,512]{1,0:T(8,128)(2,1)} %bitcast.7, bf16[64,512]{1,0:T(8,128)(2,1)} %bitcast.8, bf16[64,512]{1,0:T(8,128)(2,1)} %bitcast.9, bf16[64,1232]{1,0:T(8,128)(2,1)} %bitcast.5, bf16[64,1232]{1,0:T(8,128)(2,1)} %bitcast.6, s32[128]{0:T(128)} %img_hbm.1, f32[8,1536]{1,0:T(8,128)} %gate_hbm.1, ...), custom_call_target="tpu_custom_call" | custom-call | tf_op jit(solution)/shard_map/joint_attention/pallas_call | solution.py:384
  45.4 0.6 %copy.11 = bf16[32,1536]{1,0:T(8,128)(2,1)} copy(bf16[32,1536]{1,0:T(8,128)(2,1)S(1)} %joint_attention.1) | data formatting | bytes 196608

commit v10 on v8

--- a/solution.py
+++ b/solution.py
@@ -61,7 +61,7 @@
         pl.semaphore_signal(barrier, inc=1, device_id={"head": hpeer[s]}, device_id_type=MESH)
 
     loads = [
-        pltpu.make_async_copy(src, dst, in_s.at[n])
+        pltpu.make_async_copy(src, dst, in_s.at[2 if n == 3 else n])
         for n, (src, dst) in enumerate((
             (img_hbm, img_ref),
             (q_hbm, qt.at[0]),
@@ -203,8 +203,9 @@
     ntext = tk_hbm.shape[1]
     edge = (TSLOTS - 1) * TOK
     tail = -(-(ntext - edge) // 128) * 128
-    for cp in loads[:4]:
+    for cp in loads[:2]:
         cp.wait()
+    pltpu.make_async_copy(kv.at[0], kv.at[0], in_s.at[2]).wait()
     with jax.named_scope("barrier"):
         pl.semaphore_wait(barrier, 10)
 

time: 46.2 us -> 46.2 us (level)
  no operation moved by 1% of the time
where the time goes in v10:
time: 46.2 us; the launch traced here: 46 us
  Pallas kernels  45.4 us (98%)
  local copies, waits for them, and re-layouts  0.64 us (1%)
    pallas_call x1, Pallas kernels, on_device(): pl.pallas_call(kernel, out_shape=pltpu.VMEM((ROWS, D), BF), in_specs=[hb]...  45.4 us

profile of v10, /device:TPU:1, one launch (start us, length us, event | category | flops | bytes accessed | tf_op | source)
XLA Modules:
  0.0 46.0 jit_solution(18255180252749774272)
XLA Ops:
  0.0 45.4 %joint_attention.1 = bf16[32,1536]{1,0:T(8,128)(2,1)S(1)} custom-call(bf16[64,512]{1,0:T(8,128)(2,1)} %bitcast.7, bf16[64,512]{1,0:T(8,128)(2,1)} %bitcast.8, bf16[64,512]{1,0:T(8,128)(2,1)} %bitcast.9, bf16[64,1232]{1,0:T(8,128)(2,1)} %bitcast.5, bf16[64,1232]{1,0:T(8,128)(2,1)} %bitcast.6, s32[128]{0:T(128)} %img_hbm.1, f32[8,1536]{1,0:T(8,128)} %gate_hbm.1, ...), custom_call_target="tpu_custom_call" | custom-call | tf_op jit(solution)/shard_map/joint_attention/pallas_call | solution.py:375
  45.4 0.6 %copy.11 = bf16[32,1536]{1,0:T(8,128)(2,1)} copy(bf16[32,1536]{1,0:T(8,128)(2,1)S(1)} %joint_attention.1) | data formatting | bytes 196608
